TPU v7x, 32 devices: a whole 2x2x4 slice. The times are simulated.
32 devices in a mesh: tm: 8 (over y, x, core), space: 4 (over z).
Axes of the slice: x: 2, y: 2, z: 4, core: 2. Of those that a mesh axis runs over, the one named last changes fastest.
Arguments:
- evecs: float32 [8, 2, 3072, 256], P('tm', None, 'space'), may hold values from -0.109375 to 0.109375
- solutions: float32 [8, 2, 3072, 128], P('tm', None, 'space'), may hold values from -6 to 6
- sink_time_weight: float32 [8, 8], P(None, 'tm'), may hold values from 0.1 to 1
- noise_source_vector: float32 [8, 2, 4, 256], P('tm'), may hold values from -6 to 6
- probe: float32 [8, 2, 4, 256], P('tm'), may hold values from -6 to 6
- dilution_spin_index: int32 [8, 4], P('tm'), may hold values from 0 to 3
- dilution_lace_index: int32 [8, 4], P('tm'), may hold values from 0 to 7
Outputs:
- smeared: float32 [8, 2, 16, 3072], P('tm', None, None, 'space')
All inputs are finite; a program needn't handle non-finite values.
Results may differ from a plain program's by a relative error of at most 0.000071.
Values sent between devices are 32-bit elements; how exact they have to be, the bound alone decides.
No kernel may reach another device: no remote copies, remote signals or barrier semaphores. Data moves between devices by JAX's collectives and lax.ppermute only.
A program may use at most 64 MiB of HBM per device.

v0:
```python
import jax
import jax.numpy as jnp
from jax import lax
from jax.sharding import PartitionSpec as P

EIGEN_COUNT = 256
DILUTION_COUNT = 4
SPIN_COUNT = 4
LACE_CLASSES = 8


def row_dot(left, right):
    return lax.dot_general(
        left,
        right,
        (((0,), (0,)), ((), ())),
        precision=lax.Precision.HIGHEST,
        preferred_element_type=jnp.float32,
    )


def per_device(
    evecs,
    solutions,
    sink_time_weight,
    noise_source_vector,
    probe,
    dilution_spin_index,
    dilution_lace_index,
):
    hp = lax.Precision.HIGHEST
    vreal, vimag = (evecs[0, 0], evecs[0, 1])
    preal, pimag = (solutions[0, 0], solutions[0, 1])
    part_real = row_dot(vreal, preal) + row_dot(vimag, pimag)
    part_imag = row_dot(vreal, pimag) - row_dot(vimag, preal)
    partial_value = jnp.stack([part_real, part_imag])
    n_time = lax.axis_size("tm")
    sums = lax.psum(partial_value, "space")
    eigen_modes = sums.shape[1]
    blocks = sums.reshape(2, eigen_modes, n_time, sums.shape[2] // n_time)
    received = lax.all_to_all(blocks, "tm", split_axis=2, concat_axis=2, tiled=True)
    weights = sink_time_weight[:, 0]
    summed_result = jnp.einsum("cntj,t->cnj", received, weights, precision=hp)
    summed_result = summed_result.reshape(2, eigen_modes, DILUTION_COUNT, SPIN_COUNT)
    vector_lanes = jnp.arange(EIGEN_COUNT, dtype=jnp.int32) % LACE_CLASSES
    lace_matches = (vector_lanes[None, :] == dilution_lace_index[0][:, None]).astype(jnp.float32)
    spin_matches = (
        jnp.arange(SPIN_COUNT, dtype=jnp.int32)[None, :] == dilution_spin_index[0][:, None]
    ).astype(jnp.float32)
    ereal, eimag = (noise_source_vector[0, 0], noise_source_vector[0, 1])
    qreal, qimag = (probe[0, 0], probe[0, 1])
    prod_real = ereal * qreal + eimag * qimag
    prod_imag = ereal * qimag - eimag * qreal
    w_real = jnp.einsum("km,sm->ks", lace_matches, prod_real, precision=hp) * spin_matches
    w_imag = jnp.einsum("km,sm->ks", lace_matches, prod_imag, precision=hp) * spin_matches
    y_real, y_imag = (summed_result[0], summed_result[1])
    z_real = jnp.einsum("nka,ks->nas", y_real, w_real, precision=hp) - jnp.einsum(
        "nka,ks->nas", y_imag, w_imag, precision=hp
    )
    z_imag = jnp.einsum("nka,ks->nas", y_real, w_imag, precision=hp) + jnp.einsum(
        "nka,ks->nas", y_imag, w_real, precision=hp
    )
    combined = jnp.stack(
        [
            z_real.reshape(eigen_modes, SPIN_COUNT * SPIN_COUNT),
            z_imag.reshape(eigen_modes, SPIN_COUNT * SPIN_COUNT),
        ]
    )
    f_real = row_dot(combined[0], vreal.T) - row_dot(combined[1], vimag.T)
    f_imag = row_dot(combined[1], vreal.T) + row_dot(combined[0], vimag.T)
    return jnp.stack([f_real, f_imag])[None]


def solution(mesh):
    placed = (
        P("tm", None, "space", None),
        P("tm", None, "space", None),
        P(None, "tm"),
        P("tm", None, None, None),
        P("tm", None, None, None),
        P("tm", None),
        P("tm", None),
    )
    return jax.shard_map(
        per_device,
        mesh=mesh,
        in_specs=placed,
        out_specs=P("tm", None, None, "space"),
        check_vma=False,
    )
```

profile of v0, /device:TPU:0, one launch (start us, length us, event | category | flops | bytes accessed | tf_op | source)
XLA Modules:
  0.0 74.4 jit_solution(3639975347307049865)
XLA Ops:
  6.5 0.0 copy-start
  6.5 0.0 copy-start.1
  6.5 0.0 copy-start.2
  6.5 0.0 all-reduce.2.cloned.1.call-start
  6.5 2.2 %fusion.14 = f32[256,128]{0,1:T(8,128)S(1)} fusion(f32[1,2,768,256]{3,2,1,0:T(8,128)} %param.7, f32[1,2,768,128]{3,2,1,0:T(8,128)} %param.8), kind=kOutput, calls=%fused_computation.22 | convolution fusion | flops 301989888 | bytes 1310720 | tf_op jit(solution)/shard_map/dot_general | solution.py:13
  8.7 2.0 %fusion.16 = f32[256,128]{0,1:T(8,128)S(1)} fusion(f32[1,2,768,256]{3,2,1,0:T(8,128)} %param.7, f32[1,2,768,128]{3,2,1,0:T(8,128)} %param.8), kind=kOutput, calls=%fused_computation.24 | convolution fusion | flops 301989888 | bytes 1310720 | tf_op jit(solution)/shard_map/dot_general | solution.py:13
  10.8 0.0 copy-done.1
  10.8 0.0 copy-done.2
  10.8 0.8 %fusion = f32[1,256,128]{1,2,0:T(8,128)S(1)} fusion(f32[256,128]{0,1:T(8,128)S(1)} %fusion.14, f32[1,2,768,256]{3,2,1,0:T(8,128)S(1)} %copy-done.1, f32[1,2,768,128]{3,2,1,0:T(8,128)S(1)} %copy-done.2), kind=kOutput, calls=%fused_computation.1 | convolution fusion | flops 302022656 | bytes 1441792 | tf_op jit(solution)/shard_map/dot_general | solution.py:13
  11.7 0.0 copy-start.3
  11.7 0.0 copy-start.4
  11.7 0.0 copy-start.5
  11.7 0.0 copy-start.6
  11.7 0.8 %fusion.1 = f32[1,256,128]{1,2,0:T(8,128)S(1)} fusion(f32[256,128]{0,1:T(8,128)S(1)} %fusion.16, f32[1,2,768,256]{3,2,1,0:T(8,128)S(1)} %copy-done.1, f32[1,2,768,128]{3,2,1,0:T(8,128)S(1)} %copy-done.2), kind=kOutput, calls=%fused_computation.3 | convolution fusion | flops 302022656 | bytes 1441792 | tf_op jit(solution)/shard_map/dot_general | solution.py:13
  12.6 0.7 copy.20
  13.3 0.0 all-reduce.2.cloned.1.call-update
  13.4 38.5 %all-reduce.2.cloned.1.call-done = f32[2,256,8,16]{1,3,0,2:T(8,128)} async-done(((f32[2,256,8,16]{1,3,0,2:T(8,128)}), f32[2,256,8,16]{1,3,0,2:T(8,128)}) %all-reduce.2.cloned.1.call-update) | async-done | bytes 262160 | tf_op jit(solution)/shard_map/psum | solution.py:38
  51.8 3.7 %all-to-all-start = ((f32[2,256,8,16]{1,3,0,2:T(8,128)}), f32[2,256,8,16]{1,3,0,2:T(8,128)S(1)}, u32[]{:S(2)}, u32[]{:S(2)}) async-start(f32[2,256,8,16]{1,3,0,2:T(8,128)} %all-reduce.2.cloned.1.call-done), calls=%async_computation | async-start | bytes 524288 | tf_op jit(solution)/shard_map/all_to_all | solution.py:41
  55.5 0.0 copy-done.3
  55.5 0.0 copy-done.4
  55.5 0.0 copy-done.5
  55.5 0.0 copy-done.6
  55.5 0.2 fusion.5
  55.7 0.2 fusion.4
  55.9 6.5 %all-to-all-done = f32[2,256,8,16]{1,3,0,2:T(8,128)S(1)} async-done(((f32[2,256,8,16]{1,3,0,2:T(8,128)}), f32[2,256,8,16]{1,3,0,2:T(8,128)S(1)}, u32[]{:S(2)}, u32[]{:S(2)}) %all-to-all-start) | async-done | bytes 262176 | tf_op jit(solution)/shard_map/all_to_all | solution.py:41
  62.4 0.0 copy-done
  62.4 0.5 fusion.34
  63.0 0.2 fusion.40
  63.2 0.2 fusion.38
  63.4 0.2 convolution_subtract_fusion.2
  63.7 0.7 fusion.12
  64.4 0.2 convolution_add_fusion.2
  64.6 0.7 fusion.10
  65.4 0.7 %fusion.3 = f32[1,16,768]{2,1,0:T(8,128)S(1)} fusion(f32[16,768]{1,0:T(8,128)S(1)} %fusion.12, f32[256,16]{0,1:T(8,128)S(1)} %squeeze_stack_reshape.9, f32[1,2,768,256]{3,2,1,0:T(8,128)S(1)} %copy-done.1), kind=kOutput, calls=%fused_computation.7 | convolution fusion | flops 37761024 | bytes 901120 | tf_op jit(solution)/shard_map/dot_general | solution.py:13
  66.1 0.7 %fusion.2 = f32[1,16,768]{2,1,0:T(8,128)S(1)} fusion(f32[16,768]{1,0:T(8,128)S(1)} %fusion.10, f32[256,16]{0,1:T(8,128)S(1)} %squeeze_stack_reshape.8, f32[1,2,768,256]{3,2,1,0:T(8,128)S(1)} %copy-done.1), kind=kOutput, calls=%fused_computation.5 | convolution fusion | flops 37761024 | bytes 901120 | tf_op jit(solution)/shard_map/dot_general | solution.py:13
  66.9 0.7 maximum_bitcast_fusion
  (8 shorter events, 0.1 us)
Async XLA Ops:
  6.5 55.9 %copy-start = (f32[8,1]{0,1:T(1,128)S(1)}, f32[8,1]{0,1:T(1,128)}, u32[]{:S(2)}) copy-start(f32[8,1]{0,1:T(1,128)} %param.9) | copy-start | bytes 100
  6.5 4.3 %copy-start.1 = (f32[1,2,768,256]{3,2,1,0:T(8,128)S(1)}, f32[1,2,768,256]{3,2,1,0:T(8,128)}, u32[]{:S(2)}) copy-start(f32[1,2,768,256]{3,2,1,0:T(8,128)} %param.7) | copy-start | bytes 4718596
  6.5 4.3 %copy-start.2 = (f32[1,2,768,128]{3,2,1,0:T(8,128)S(1)}, f32[1,2,768,128]{3,2,1,0:T(8,128)}, u32[]{:S(2)}) copy-start(f32[1,2,768,128]{3,2,1,0:T(8,128)} %param.8) | copy-start | bytes 2359300
  6.5 45.3 %all-reduce.2.cloned.1.call-start = ((), (), s32[]{:S(2)}) async-start(), calls=%async_computation.1 | async-start | bytes 524288 | tf_op jit(solution)/shard_map/psum | solution.py:38
  11.7 43.8 %copy-start.3 = (f32[1,2,4,256]{3,2,1,0:T(4,128)S(1)}, f32[1,2,4,256]{3,2,1,0:T(4,128)}, u32[]{:S(2)}) copy-start(f32[1,2,4,256]{3,2,1,0:T(4,128)} %param.11) | copy-start | bytes 24580
  11.7 43.8 %copy-start.4 = (f32[1,2,4,256]{3,2,1,0:T(4,128)S(1)}, f32[1,2,4,256]{3,2,1,0:T(4,128)}, u32[]{:S(2)}) copy-start(f32[1,2,4,256]{3,2,1,0:T(4,128)} %param.10) | copy-start | bytes 24580
  11.7 43.8 %copy-start.5 = (s32[1,4]{1,0:T(1,128)S(1)}, s32[1,4]{1,0:T(1,128)}, u32[]{:S(2)}) copy-start(s32[1,4]{1,0:T(1,128)} %param.13) | copy-start | bytes 52
  11.7 43.8 %copy-start.6 = (s32[1,4]{1,0:T(1,128)S(1)}, s32[1,4]{1,0:T(1,128)}, u32[]{:S(2)}) copy-start(s32[1,4]{1,0:T(1,128)} %param.12) | copy-start | bytes 52
  51.8 10.6 %all-to-all-start = ((f32[2,256,8,16]{1,3,0,2:T(8,128)}), f32[2,256,8,16]{1,3,0,2:T(8,128)S(1)}, u32[]{:S(2)}, u32[]{:S(2)}) async-start(f32[2,256,8,16]{1,3,0,2:T(8,128)} %all-reduce.2.cloned.1.call-done), calls=%async_computation | async-start | bytes 524288 | tf_op jit(solution)/shard_map/all_to_all | solution.py:41
Sparse Core Ops, SparseCore 0:
  13.5 38.3 all-reduce.1
where the time goes:
time: 74.6 us; the launch traced here: 74.4 us
  waiting for transfers between devices  45 us (60%)
  between operations  13.6 us (18%)
  matrix products  10.7 us (14%)
  starting transfers between devices  3.66 us (5%)
  local copies, waits for them, and re-layouts  0.81 us (1%)
    psum x1, waiting for transfers between devices, per_device(): sums = lax.psum(partial_value, 'space')  38.5 us
    dot_general x8, matrix products, row_dot(): lax.dot_general(left, right, (((0,), (0,)), ((), ())), precision=lax.Prec...  8.88 us
    all_to_all x1, waiting for transfers between devices, per_device(): lax.all_to_all(blocks, 'tm', split_axis=2, concat_axis=2, tiled=True)  6.5 us
    all_to_all x1, starting transfers between devices, per_device(): lax.all_to_all(blocks, 'tm', split_axis=2, concat_axis=2, tiled=True)  3.66 us
  transfers between devices with their start and end apart: 2, of which 2 were waited for; matrix products, arithmetic and copies ran while one was open for 1% of the time, Pallas kernels for 0%

commit v1 on v0

v1 whole, which is shorter than its diff:
```python
import functools

import jax
import jax.numpy as jnp
from jax import lax
from jax.experimental import pallas as pl
from jax.experimental.pallas import tpu as pltpu
from jax.sharding import PartitionSpec as P

LACE_CLASSES = 8
SPIN_COUNT = 4
BF16 = jnp.bfloat16
F32 = jnp.float32
VMEM_SPEC = pl.BlockSpec(memory_space=pltpu.VMEM)
SMEM_SPEC = pl.BlockSpec(memory_space=pltpu.SMEM)


def split(x):
    high = x.astype(BF16)
    low = (x - high.astype(F32)).astype(BF16)
    return high, low


def dot3(left, right, contract=((1,), (0,))):
    lh, ll = left
    rh, rl = right
    mul = functools.partial(
        lax.dot_general, dimension_numbers=(contract, ((), ())), preferred_element_type=F32
    )
    rows = lh.shape[0]
    both = mul(jnp.concatenate([lh, ll], 0), rh)
    return both[:rows] + both[rows:] + mul(lh, rl)


def project_kernel(chips, index_ref, evecs_ref, solutions_ref, keep_ref, send_ref, total_ref):
    step = pl.program_id(0)
    rows, modes = evecs_ref.shape[2:]
    cols = solutions_ref.shape[3]
    half = cols // (2 * chips)
    real = solutions_ref[0, 0].T
    imag = solutions_ref[0, 1].T
    left = jnp.concatenate(
        [jnp.concatenate([real, imag], 0), jnp.concatenate([imag, -real], 0)], 1
    )
    right = evecs_ref[0].reshape(2 * rows, modes)
    value = dot3(split(left), split(right))

    @pl.when(step == 0)
    def _():
        total_ref[...] = value

    @pl.when(step > 0)
    def _():
        total_ref[...] += value

    @pl.when(step == pl.num_programs(0) - 1)
    def _():
        for out, base in ((keep_ref, 0), (send_ref, chips)):
            for m in range(chips):
                block = index_ref[base + m]
                for part in range(2):
                    start = pl.multiple_of(part * cols + block * half, 8)
                    out[m, part * half : (part + 1) * half] = total_ref[pl.ds(start, half)]


def project(evecs, solutions, blocks, chips):
    rows, modes = evecs.shape[2:]
    cols = solutions.shape[3]
    block_rows = 2 * cols // (2 * chips)
    step = 256 if rows % 256 == 0 else rows
    out = jax.ShapeDtypeStruct((chips, block_rows, modes), F32)
    whole = pl.BlockSpec((chips, block_rows, modes), lambda i, s: (0, 0, 0))
    return pl.pallas_call(
        functools.partial(project_kernel, chips),
        grid_spec=pltpu.PrefetchScalarGridSpec(
            num_scalar_prefetch=1,
            grid=(rows // step,),
            in_specs=[
                pl.BlockSpec((1, 2, step, modes), lambda i, s: (0, 0, i, 0)),
                pl.BlockSpec((1, 2, step, cols), lambda i, s: (0, 0, i, 0)),
            ],
            out_specs=[whole, whole],
            scratch_shapes=[pltpu.VMEM((2 * cols, modes), F32)],
        ),
        out_shape=[out, out],
        name="project",
    )(blocks, evecs, solutions)


def mixing_matrix(noise_ref, probe_ref, spin_ref, lace_ref, width):
    noise_real, noise_imag = noise_ref[0, 0], noise_ref[0, 1]
    probe_real, probe_imag = probe_ref[0, 0], probe_ref[0, 1]
    prod_real = noise_real * probe_real + noise_imag * probe_imag
    prod_imag = noise_real * probe_imag - noise_imag * probe_real
    spins, modes = prod_real.shape
    groups = width // spins
    prod = jnp.concatenate([prod_real] * groups + [prod_imag] * groups, 0)
    lanes = lax.broadcasted_iota(jnp.int32, (2 * width, modes), 1) % LACE_CLASSES
    row = lax.broadcasted_iota(jnp.int32, (2 * width, width), 0) % width
    col = lax.broadcasted_iota(jnp.int32, (2 * width, width), 1)
    same = (row // spins) == (col % groups)
    both = jnp.zeros((2 * width, width), F32)
    for k in range(width // groups):
        picked = jnp.sum(jnp.where(lanes == lace_ref[0, k], prod, 0.0), axis=1, keepdims=True)
        on = same & ((col // groups) == k) & ((row % spins) == spin_ref[0, k])
        both = both + jnp.where(on, picked, 0.0)
    real, imag = both[:width], both[width:]
    return jnp.concatenate(
        [jnp.concatenate([real, -imag], 1), jnp.concatenate([imag, real], 1)], 0
    )


def recombine_kernel(copies, masks, me_ref, weight_ref, noise_ref, probe_ref, spin_ref, lace_ref, *refs):
    keep_ref, recv_ref = refs[:2]
    others, out_ref = refs[2:-1], refs[-1]
    me = me_ref[0]
    total = keep_ref[0] * weight_ref[me, 0] + recv_ref[0] * weight_ref[me ^ 1, 0]
    for mask, ref in zip(masks, others):
        total += ref[0] * weight_ref[me ^ mask, 0] + ref[1] * weight_ref[me ^ mask ^ 1, 0]
    mix = mixing_matrix(noise_ref, probe_ref, spin_ref, lace_ref, total.shape[0] // 2)
    value = dot3(split(mix), split(total))
    for i in range(copies):
        out_ref[i] = value


def smear_kernel(evecs_ref, parts_ref, out_ref):
    total = parts_ref[0]
    for i in range(1, parts_ref.shape[0]):
        total += parts_ref[i]
    width = total.shape[0] // 2
    turned = jnp.concatenate([-total[width:], total[:width]], 0)
    value = dot3(split(total), split(evecs_ref[0, 0]), ((1,), (1,)))
    value += dot3(split(turned), split(evecs_ref[0, 1]), ((1,), (1,)))
    out_ref[0, 0] = value[:width]
    out_ref[0, 1] = value[width:]


def per_device(
    evecs,
    solutions,
    sink_time_weight,
    noise_source_vector,
    probe,
    dilution_spin_index,
    dilution_lace_index,
):
    n_time, n_space = lax.axis_size("tm"), lax.axis_size("space")
    rows, modes = evecs.shape[2:]
    width = solutions.shape[3] // n_time
    chips = n_time // 2
    me = lax.axis_index("tm").astype(jnp.int32)
    masks = [2 * m + bin(m).count("1") % 2 for m in range(chips)]
    blocks = me ^ jnp.array(masks + [mask ^ 1 for mask in masks], jnp.int32)
    keep, send = project(evecs, solutions, blocks, chips)

    def swap(value, mask):
        return lax.ppermute(value, "tm", [(i, i ^ mask) for i in range(n_time)])

    recv = swap(send, 1)
    pairs = [jnp.stack([keep[m], recv[m]]) for m in range(1, chips)]
    others = [swap(pair, mask) for pair, mask in zip(pairs, masks[1:])]
    block = (2 * width, modes)
    parts = pl.pallas_call(
        functools.partial(recombine_kernel, n_space, masks[1:]),
        in_specs=[SMEM_SPEC, SMEM_SPEC, VMEM_SPEC, VMEM_SPEC, SMEM_SPEC, SMEM_SPEC]
        + [VMEM_SPEC] * (chips + 1),
        out_specs=VMEM_SPEC,
        out_shape=jax.ShapeDtypeStruct((n_space,) + block, F32),
        name="recombine",
    )(
        me[None],
        sink_time_weight,
        noise_source_vector,
        probe,
        dilution_spin_index,
        dilution_lace_index,
        keep[:1],
        recv[:1],
        *others,
    )
    parts = lax.all_to_all(parts, "space", 0, 0, tiled=True)
    return pl.pallas_call(
        smear_kernel,
        in_specs=[VMEM_SPEC, VMEM_SPEC],
        out_specs=VMEM_SPEC,
        out_shape=jax.ShapeDtypeStruct((1, 2, width, rows), F32),
        name="smear",
    )(evecs, parts)


def solution(mesh):
    placed = (
        P("tm", None, "space", None),
        P("tm", None, "space", None),
        P(None, "tm"),
        P("tm", None, None, None),
        P("tm", None, None, None),
        P("tm", None),
        P("tm", None),
    )
    return jax.shard_map(
        per_device,
        mesh=mesh,
        in_specs=placed,
        out_specs=P("tm", None, None, "space"),
        check_vma=False,
    )
```

time: 74.6 us -> 33 us (0.44)
  waiting for transfers between devices: 45 us -> 3.07 us
  between operations: 13.6 us -> 0.02 us
  blocking collectives: 0 us -> 11.4 us
  matrix products: 10.7 us -> 0 us
  Pallas kernels: 0 us -> 9.22 us
  local copies, waits for them, and re-layouts: 0.81 us -> 3.36 us
  starting transfers between devices: 3.66 us -> 4.41 us
    psum x1 -> x0, waiting for transfers between devices: 38.5 us -> none  [per_device(): sums = lax.psum(partial_value, 'space')]
    all_to_all x0 -> x1, blocking collectives: none -> 11.4 us  [per_device(): parts = lax.all_to_all(parts, 'space', 0, 0, tiled=True)]
    dot_general x15 -> x0, matrix products: 10.7 us -> none  [the longest x8 8.88 us: row_dot(): lax.dot_general(left, right, (((0,), (0,)), ((), ())), precision=lax.Prec...]
    pallas_call x0 -> x3, Pallas kernels: none -> 9.22 us  [the longest x1 4.68 us: project(): pl.pallas_call(functools.partial(project_kernel, chips), grid_spec=pltpu....]
    all_to_all x1 -> x0, waiting for transfers between devices: 6.5 us -> none  [per_device(): lax.all_to_all(blocks, 'tm', split_axis=2, concat_axis=2, tiled=True)]
    ppermute x0 -> x4, starting transfers between devices: none -> 4.41 us  [swap(): return lax.ppermute(value, 'tm', [(i, i ^ mask) for i in range(n_time)])]
    all_to_all x1 -> x0, starting transfers between devices: 3.66 us -> none  [per_device(): lax.all_to_all(blocks, 'tm', split_axis=2, concat_axis=2, tiled=True)]
    ppermute x0 -> x4, waiting for transfers between devices: none -> 3.07 us  [swap(): return lax.ppermute(value, 'tm', [(i, i ^ mask) for i in range(n_time)])]
  transfers between devices with their start and end apart: 2 -> 4, of which waited for: 2 -> 2; matrix products, arithmetic and copies ran while one was open for 1% -> 6% of each run, Pallas kernels for 0% -> 0%
where the time goes in v1:
time: 33 us; the launch traced here: 32.6 us
  blocking collectives  11.4 us (35%)
  Pallas kernels  9.22 us (28%)
  starting transfers between devices  4.41 us (13%)
  local copies, waits for them, and re-layouts  3.36 us (10%)
  waiting for transfers between devices  3.07 us (9%)
  other arithmetic  1.18 us (4%)
    all_to_all x1, blocking collectives, per_device(): parts = lax.all_to_all(parts, 'space', 0, 0, tiled=True)  11.4 us
    pallas_call x1, Pallas kernels, project(): pl.pallas_call(functools.partial(project_kernel, chips), grid_spec=pltpu....  4.68 us
    ppermute x4, starting transfers between devices, swap(): return lax.ppermute(value, 'tm', [(i, i ^ mask) for i in range(n_time)])  4.41 us
    ppermute x4, waiting for transfers between devices, swap(): return lax.ppermute(value, 'tm', [(i, i ^ mask) for i in range(n_time)])  3.07 us
    pallas_call x1, Pallas kernels, per_device(): pl.pallas_call(smear_kernel, in_specs=[VMEM_SPEC, VMEM_SPEC], out_specs=V...  2.63 us
    slice x2, local copies, waits for them, and re-layouts, per_device(): pairs = [jnp.stack([keep[m], recv[m]]) for m in range(1, chips)]  2.04 us
    pallas_call x1, Pallas kernels, per_device(): pl.pallas_call(functools.partial(recombine_kernel, n_space, masks[1:]), i...  1.92 us
    unnamed x9, local copies, waits for them, and re-layouts  1.31 us
  transfers between devices with their start and end apart: 4, of which 2 were waited for; matrix products, arithmetic and copies ran while one was open for 6% of the time, Pallas kernels for 0%

profile of v1, /device:TPU:0, one launch (start us, length us, event | category | flops | bytes accessed | tf_op | source)
XLA Modules:
  0.0 32.6 jit_solution(1729579514740812328)
XLA Ops:
  0.0 1.2 %broadcast_xor_fusion.index_ref = s32[8]{0:T(128)} fusion(s32[8]{0:T(128)} %constant.8.clone, s32[]{:T(128)} %axis_index.15), kind=kLoop, calls=%fused_computation.3 | loop fusion | flops 8 | bytes 68 | tf_op jit(solution)/shard_map/xor | solution.py:153
  1.2 0.0 copy-start.3
  1.2 4.7 %project.1 = (f32[4,32,256]{2,1,0:T(8,128)}, f32[4,32,256]{2,1,0:T(8,128)}) custom-call(s32[8]{0:T(128)} %broadcast_xor_fusion.index_ref, f32[1,2,768,256]{3,2,1,0:T(8,128)} %evecs_ref.3, f32[1,2,768,128]{3,2,1,0:T(8,128)} %solutions_ref.1), custom_call_target="tpu_custom_call" | custom-call | tf_op jit(solution)/shard_map/project/pallas_call | solution.py:73
  5.8 0.5 %collective-permute-start = (f32[4,32,256]{2,1,0:T(8,128)}, f32[4,32,256]{2,1,0:T(8,128)S(1)}, u32[]{:S(2)}, u32[]{:S(2)}) collective-permute-start(f32[4,32,256]{2,1,0:T(8,128)} %get-tuple-element.8), channel_id=1, source_target_pairs={{0,4},{4,0},{8,12},{12,8},{16,20},{20,16},{24,28},{28,24},{1,5},{5... | collective-permute-start | bytes 393224 | tf_op jit(solution)/shard_map/ppermute | solution.py:157
  6.3 1.4 %fusion = (f32[1,32,256]{2,1,0:T(8,128)S(1)}, f32[1,32,256]{2,1,0:T(8,128)S(1)}, f32[1,32,256]{2,1,0:T(8,128)S(1)}, f32[1,32,256]{2,1,0:T(8,128)}) fusion(f32[4,32,256]{2,1,0:T(8,128)} %get-tuple-element.7), kind=kLoop, calls=%fused_computation.4 | loop fusion | bytes 262144 | tf_op jit(solution)/shard_map/slice | solution.py:160
  7.8 0.0 collective-permute-done
  7.8 0.6 %fusion.1 = (f32[1,32,256]{2,1,0:T(8,128)S(1)}, f32[1,32,256]{2,1,0:T(8,128)S(1)}, f32[1,32,256]{2,1,0:T(8,128)S(1)}, f32[1,32,256]{2,1,0:T(8,128)}) fusion(f32[4,32,256]{2,1,0:T(8,128)S(1)} %collective-permute-done), kind=kLoop, calls=%fused_computation.5 | loop fusion | bytes 262144 | tf_op jit(solution)/shard_map/slice | solution.py:160
  8.4 3.6 %collective-permute-start.3 = (f32[2,32,256]{2,1,0:T(8,128)S(1)}, f32[2,32,256]{2,1,0:T(8,128)S(1)}, u32[]{:S(2)}, u32[]{:S(2)}) collective-permute-start(f32[2,32,256]{2,1,0:T(8,128)S(1)} %pad_maximum_fusion.2), channel_id=1, source_target_pairs={{0,24},{4,28},{8,16},{12,20},{16,8},{20,12},{24,0},{28,4},{1,25},{... | collective-permute-start | bytes 196616 | tf_op jit(solution)/shard_map/ppermute | solution.py:157
  12.0 0.2 collective-permute-start.2
  12.2 0.1 collective-permute-start.1
  12.3 0.0 copy-done.3
  12.3 0.7 %copy.9.weight_ref = f32[8,1]{1,0:T(8,128)} copy(f32[8,1]{0,1:T(1,128)S(1)} %copy-done.3) | data formatting | bytes 64 | tf_op args[2]
  13.0 1.6 %collective-permute-done.3.refs_4_ = f32[2,32,256]{2,1,0:T(8,128)S(1)} collective-permute-done((f32[2,32,256]{2,1,0:T(8,128)S(1)}, f32[2,32,256]{2,1,0:T(8,128)S(1)}, u32[]{:S(2)}, u32[]{:S(2)}) %collective-permute-start.3) | collective-permute-done | bytes 65568 | tf_op jit(solution)/shard_map/ppermute | solution.py:157
  14.6 0.0 copy-start
  14.6 1.5 %collective-permute-done.2.refs_3_ = f32[2,32,256]{2,1,0:T(8,128)S(1)} collective-permute-done((f32[2,32,256]{2,1,0:T(8,128)S(1)}, f32[2,32,256]{2,1,0:T(8,128)S(1)}, u32[]{:S(2)}, u32[]{:S(2)}) %collective-permute-start.2) | collective-permute-done | bytes 65568 | tf_op jit(solution)/shard_map/ppermute | solution.py:157
  16.1 0.0 copy-start.1
  16.1 0.0 collective-permute-done.1.refs_2_
  16.1 0.0 copy-start.2
  16.1 0.0 copy-done
  16.1 0.6 %copy-done.1 = f32[2,32,256]{2,1,0:T(8,128)} copy-done((f32[2,32,256]{2,1,0:T(8,128)}, f32[2,32,256]{2,1,0:T(8,128)S(1)}, u32[]{:S(2)}) %copy-start.1) | copy-done | bytes 65560
  16.7 0.0 copy-done.2
  16.7 1.9 %recombine.1 = f32[4,32,256]{2,1,0:T(8,128)} custom-call(s32[1]{0:T(128)} %bitcast.me_ref, f32[8,1]{1,0:T(8,128)} %copy.9.weight_ref, f32[1,2,4,256]{3,2,1,0:T(4,128)} %noise_ref.1, f32[1,2,4,256]{3,2,1,0:T(4,128)} %probe_ref.1, s32[1,4]{1,0:T(1,128)} %spin_ref.1, s32[1,4]{1,0:T(1,128)} %lace_ref.1, f32[1,32,256]{2,1,0:T(8,128)} %get-tuple-element.12.refs_0_, ...), custom_call_target="tpu_custom_call" | custom-call | tf_op jit(solution)/shard_map/recombine/pallas_call | solution.py:163
  18.6 11.4 %all_to_all.5.parts_ref = f32[4,32,256]{2,1,0:T(8,128)} all-to-all(f32[4,32,256]{2,1,0:T(8,128)} %recombine.1), channel_id=1, replica_groups=mesh['tm'=8,'space'=4] {'space'}, dimensions={0} | all-to-all | bytes 262144 | tf_op jit(solution)/shard_map/all_to_all | solution.py:181
  30.0 2.6 %smear.1 = f32[1,2,16,768]{3,2,1,0:T(8,128)} custom-call(f32[1,2,768,256]{3,2,1,0:T(8,128)} %evecs_ref.3, f32[4,32,256]{2,1,0:T(8,128)} %all_to_all.5.parts_ref), custom_call_target="tpu_custom_call" | custom-call | tf_op jit(solution)/shard_map/smear/pallas_call | solution.py:182
  (3 shorter events, 0.0 us)
Async XLA Ops:
  1.2 11.2 %copy-start.3 = (f32[8,1]{0,1:T(1,128)S(1)}, f32[8,1]{0,1:T(1,128)}, u32[]{:S(2)}) copy-start(f32[8,1]{0,1:T(1,128)} %param.10) | copy-start | bytes 100
  5.8 1.9 %collective-permute-start = (f32[4,32,256]{2,1,0:T(8,128)}, f32[4,32,256]{2,1,0:T(8,128)S(1)}, u32[]{:S(2)}, u32[]{:S(2)}) collective-permute-start(f32[4,32,256]{2,1,0:T(8,128)} %get-tuple-element.8), channel_id=1, source_target_pairs={{0,4},{4,0},{8,12},{12,8},{16,20},{20,16},{24,28},{28,24},{1,5},{5... | collective-permute-start | bytes 393224 | tf_op jit(solution)/shard_map/ppermute | solution.py:157
  8.4 6.2 %collective-permute-start.3 = (f32[2,32,256]{2,1,0:T(8,128)S(1)}, f32[2,32,256]{2,1,0:T(8,128)S(1)}, u32[]{:S(2)}, u32[]{:S(2)}) collective-permute-start(f32[2,32,256]{2,1,0:T(8,128)S(1)} %pad_maximum_fusion.2), channel_id=1, source_target_pairs={{0,24},{4,28},{8,16},{12,20},{16,8},{20,12},{24,0},{28,4},{1,25},{... | collective-permute-start | bytes 196616 | tf_op jit(solution)/shard_map/ppermute | solution.py:157
  12.0 4.1 %collective-permute-start.2 = (f32[2,32,256]{2,1,0:T(8,128)S(1)}, f32[2,32,256]{2,1,0:T(8,128)S(1)}, u32[]{:S(2)}, u32[]{:S(2)}) collective-permute-start(f32[2,32,256]{2,1,0:T(8,128)S(1)} %pad_maximum_fusion.1), channel_id=1, source_target_pairs={{0,20},{4,16},{8,28},{12,24},{16,4},{20,0},{24,12},{28,8},{1,21},{... | collective-permute-start | bytes 196616 | tf_op jit(solution)/shard_map/ppermute | solution.py:157
  12.2 3.9 %collective-permute-start.1 = (f32[2,32,256]{2,1,0:T(8,128)S(1)}, f32[2,32,256]{2,1,0:T(8,128)S(1)}, u32[]{:S(2)}, u32[]{:S(2)}) collective-permute-start(f32[2,32,256]{2,1,0:T(8,128)S(1)} %pad_maximum_fusion), channel_id=1, source_target_pairs={{0,12},{4,8},{8,4},{12,0},{16,28},{20,24},{24,20},{28,16},{1,13},{... | collective-permute-start | bytes 196616 | tf_op jit(solution)/shard_map/ppermute | solution.py:157
  14.6 1.5 %copy-start = (f32[2,32,256]{2,1,0:T(8,128)}, f32[2,32,256]{2,1,0:T(8,128)S(1)}, u32[]{:S(2)}) copy-start(f32[2,32,256]{2,1,0:T(8,128)S(1)} %collective-permute-done.3.refs_4_) | copy-start | bytes 196612
  16.1 0.6 %copy-start.1 = (f32[2,32,256]{2,1,0:T(8,128)}, f32[2,32,256]{2,1,0:T(8,128)S(1)}, u32[]{:S(2)}) copy-start(f32[2,32,256]{2,1,0:T(8,128)S(1)} %collective-permute-done.2.refs_3_) | copy-start | bytes 196612
  16.1 0.6 %copy-start.2 = (f32[2,32,256]{2,1,0:T(8,128)}, f32[2,32,256]{2,1,0:T(8,128)S(1)}, u32[]{:S(2)}) copy-start(f32[2,32,256]{2,1,0:T(8,128)S(1)} %collective-permute-done.1.refs_2_) | copy-start | bytes 196612

commit v2 on v1

--- a/solution.py
+++ b/solution.py
@@ -32,8 +32,10 @@
     return both[:rows] + both[rows:] + mul(lh, rl)
 
 
-def project_kernel(chips, index_ref, evecs_ref, solutions_ref, keep_ref, send_ref, total_ref):
+def project_kernel(masks, evecs_ref, solutions_ref, keep_ref, send_ref, total_ref):
     step = pl.program_id(0)
+    chips = len(masks)
+    me = lax.axis_index("tm").astype(jnp.int32)
     rows, modes = evecs_ref.shape[2:]
     cols = solutions_ref.shape[3]
     half = cols // (2 * chips)
@@ -55,36 +57,35 @@
 
     @pl.when(step == pl.num_programs(0) - 1)
     def _():
-        for out, base in ((keep_ref, 0), (send_ref, chips)):
-            for m in range(chips):
-                block = index_ref[base + m]
+        for out, core in ((keep_ref, 0), (send_ref, 1)):
+            for m, mask in enumerate(masks):
+                block = me ^ (mask ^ core)
                 for part in range(2):
                     start = pl.multiple_of(part * cols + block * half, 8)
                     out[m, part * half : (part + 1) * half] = total_ref[pl.ds(start, half)]
 
 
-def project(evecs, solutions, blocks, chips):
+def project(evecs, solutions, masks):
+    chips = len(masks)
     rows, modes = evecs.shape[2:]
     cols = solutions.shape[3]
     block_rows = 2 * cols // (2 * chips)
     step = 256 if rows % 256 == 0 else rows
     out = jax.ShapeDtypeStruct((chips, block_rows, modes), F32)
-    whole = pl.BlockSpec((chips, block_rows, modes), lambda i, s: (0, 0, 0))
+    whole = pl.BlockSpec((chips, block_rows, modes), lambda i: (0, 0, 0))
     return pl.pallas_call(
-        functools.partial(project_kernel, chips),
-        grid_spec=pltpu.PrefetchScalarGridSpec(
-            num_scalar_prefetch=1,
-            grid=(rows // step,),
-            in_specs=[
-                pl.BlockSpec((1, 2, step, modes), lambda i, s: (0, 0, i, 0)),
-                pl.BlockSpec((1, 2, step, cols), lambda i, s: (0, 0, i, 0)),
-            ],
-            out_specs=[whole, whole],
-            scratch_shapes=[pltpu.VMEM((2 * cols, modes), F32)],
-        ),
+        functools.partial(project_kernel, masks),
+        grid=(rows // step,),
+        in_specs=[
+            pl.BlockSpec((1, 2, step, modes), lambda i: (0, 0, i, 0)),
+            pl.BlockSpec((1, 2, step, cols), lambda i: (0, 0, i, 0)),
+        ],
+        out_specs=[whole, whole],
+        scratch_shapes=[pltpu.VMEM((2 * cols, modes), F32)],
         out_shape=[out, out],
+        compiler_params=pltpu.CompilerParams(vmem_limit_bytes=32 << 20),
         name="project",
-    )(blocks, evecs, solutions)
+    )(evecs, solutions)
 
 
 def mixing_matrix(noise_ref, probe_ref, spin_ref, lace_ref, width):
@@ -110,23 +111,22 @@
     )
 
 
-def recombine_kernel(copies, masks, me_ref, weight_ref, noise_ref, probe_ref, spin_ref, lace_ref, *refs):
+def recombine_kernel(masks, weight_ref, noise_ref, probe_ref, spin_ref, lace_ref, *refs):
     keep_ref, recv_ref = refs[:2]
     others, out_ref = refs[2:-1], refs[-1]
-    me = me_ref[0]
-    total = keep_ref[0] * weight_ref[me, 0] + recv_ref[0] * weight_ref[me ^ 1, 0]
+    me = lax.axis_index("tm").astype(jnp.int32)
+    total = keep_ref[0] * weight_ref[0, me] + recv_ref[0] * weight_ref[0, me ^ 1]
     for mask, ref in zip(masks, others):
-        total += ref[0] * weight_ref[me ^ mask, 0] + ref[1] * weight_ref[me ^ mask ^ 1, 0]
+        total += ref[0] * weight_ref[0, me ^ mask] + ref[1] * weight_ref[0, me ^ mask ^ 1]
     mix = mixing_matrix(noise_ref, probe_ref, spin_ref, lace_ref, total.shape[0] // 2)
-    value = dot3(split(mix), split(total))
-    for i in range(copies):
-        out_ref[i] = value
-
-
-def smear_kernel(evecs_ref, parts_ref, out_ref):
-    total = parts_ref[0]
-    for i in range(1, parts_ref.shape[0]):
-        total += parts_ref[i]
+    out_ref[...] = dot3(split(mix), split(total))
+
+
+def smear_kernel(evecs_ref, part_ref, *refs):
+    out_ref = refs[-1]
+    total = part_ref[...]
+    for ref in refs[:-1]:
+        total += ref[...]
     width = total.shape[0] // 2
     turned = jnp.concatenate([-total[width:], total[:width]], 0)
     value = dot3(split(total), split(evecs_ref[0, 0]), ((1,), (1,)))
@@ -148,28 +148,26 @@
     rows, modes = evecs.shape[2:]
     width = solutions.shape[3] // n_time
     chips = n_time // 2
-    me = lax.axis_index("tm").astype(jnp.int32)
     masks = [2 * m + bin(m).count("1") % 2 for m in range(chips)]
-    blocks = me ^ jnp.array(masks + [mask ^ 1 for mask in masks], jnp.int32)
-    keep, send = project(evecs, solutions, blocks, chips)
-
-    def swap(value, mask):
-        return lax.ppermute(value, "tm", [(i, i ^ mask) for i in range(n_time)])
-
-    recv = swap(send, 1)
+    keep, send = project(evecs, solutions, masks)
+
+    def swap(value, axis, mask):
+        size = lax.axis_size(axis)
+        return lax.ppermute(value, axis, [(i, i ^ mask) for i in range(size)])
+
+    recv = swap(send, "tm", 1)
     pairs = [jnp.stack([keep[m], recv[m]]) for m in range(1, chips)]
-    others = [swap(pair, mask) for pair, mask in zip(pairs, masks[1:])]
-    block = (2 * width, modes)
-    parts = pl.pallas_call(
-        functools.partial(recombine_kernel, n_space, masks[1:]),
-        in_specs=[SMEM_SPEC, SMEM_SPEC, VMEM_SPEC, VMEM_SPEC, SMEM_SPEC, SMEM_SPEC]
+    others = [swap(pair, "tm", mask) for pair, mask in zip(pairs, masks[1:])]
+    part = pl.pallas_call(
+        functools.partial(recombine_kernel, masks[1:]),
+        in_specs=[SMEM_SPEC, VMEM_SPEC, VMEM_SPEC, SMEM_SPEC, SMEM_SPEC]
         + [VMEM_SPEC] * (chips + 1),
         out_specs=VMEM_SPEC,
-        out_shape=jax.ShapeDtypeStruct((n_space,) + block, F32),
+        out_shape=jax.ShapeDtypeStruct((2 * width, modes), F32),
+        compiler_params=pltpu.CompilerParams(vmem_limit_bytes=8 << 20),
         name="recombine",
     )(
-        me[None],
-        sink_time_weight,
+        sink_time_weight.T,
         noise_source_vector,
         probe,
         dilution_spin_index,
@@ -178,14 +176,15 @@
         recv[:1],
         *others,
     )
-    parts = lax.all_to_all(parts, "space", 0, 0, tiled=True)
+    parts = [swap(part, "space", mask) for mask in range(1, n_space)]
     return pl.pallas_call(
         smear_kernel,
-        in_specs=[VMEM_SPEC, VMEM_SPEC],
+        in_specs=[VMEM_SPEC] * (n_space + 1),
         out_specs=VMEM_SPEC,
         out_shape=jax.ShapeDtypeStruct((1, 2, width, rows), F32),
+        compiler_params=pltpu.CompilerParams(vmem_limit_bytes=16 << 20),
         name="smear",
-    )(evecs, parts)
+    )(evecs, part, *parts)
 
 
 def solution(mesh):

time: 33 us -> 25.9 us (0.78)
  blocking collectives: 11.4 us -> 0 us
  waiting for transfers between devices: 3.07 us -> 10.1 us
  Pallas kernels: 9.22 us -> 3.7 us
  starting transfers between devices: 4.41 us -> 9.22 us
  other arithmetic: 1.18 us -> 0.02 us
  local copies, waits for them, and re-layouts: 3.36 us -> 2.58 us
    all_to_all x1 -> x0, blocking collectives: 11.4 us -> none  [per_device(): parts = lax.all_to_all(parts, 'space', 0, 0, tiled=True)]
    ppermute x4 -> x7, waiting for transfers between devices: 3.07 us -> 10.1 us  [swap(): return lax.ppermute(value, axis, [(i, i ^ mask) for i in range(size)])]
    pallas_call x3, Pallas kernels: 9.22 us -> 3.7 us  [the longest x1 1.64 us: project(): pl.pallas_call(functools.partial(project_kernel, masks), grid=(rows // st...]
    ppermute x4 -> x7, starting transfers between devices: 4.41 us -> 9.22 us  [swap(): return lax.ppermute(value, axis, [(i, i ^ mask) for i in range(size)])]
    slice x2, local copies, waits for them, and re-layouts: 2.04 us -> 0.02 us  [per_device(): pairs = [jnp.stack([keep[m], recv[m]]) for m in range(1, chips)]]
    unnamed x9 -> x14, local copies, waits for them, and re-layouts: 1.31 us -> 2.56 us
    xor x1 -> x0, other arithmetic: 1.17 us -> none  [per_device(): blocks = me ^ jnp.array(masks + [mask ^ 1 for mask in masks], jnp.int32)]
  transfers between devices with their start and end apart: 4 -> 7, of which waited for: 2 -> 6; matrix products, arithmetic and copies ran while one was open for 6% -> 0% of each run, Pallas kernels for 0% -> 0%
where the time goes in v2:
time: 25.9 us; the launch traced here: 25.7 us
  waiting for transfers between devices  10.1 us (39%)
  starting transfers between devices  9.22 us (36%)
  Pallas kernels  3.7 us (14%)
  local copies, waits for them, and re-layouts  2.58 us (10%)
    ppermute x7, waiting for transfers between devices, swap(): return lax.ppermute(value, axis, [(i, i ^ mask) for i in range(size)])  10.1 us
    ppermute x7, starting transfers between devices, swap(): return lax.ppermute(value, axis, [(i, i ^ mask) for i in range(size)])  9.22 us
    unnamed x14, local copies, waits for them, and re-layouts  2.56 us
    pallas_call x1, Pallas kernels, project(): pl.pallas_call(functools.partial(project_kernel, masks), grid=(rows // st...  1.64 us
    pallas_call x1, Pallas kernels, per_device(): pl.pallas_call(smear_kernel, in_specs=[VMEM_SPEC] * (n_space + 1), out_sp...  1.22 us
    pallas_call x1, Pallas kernels, per_device(): pl.pallas_call(functools.partial(recombine_kernel, masks[1:]), in_specs=[...  0.84 us
  transfers between devices with their start and end apart: 7, of which 6 were waited for; matrix products, arithmetic and copies ran while one was open for 0% of the time, Pallas kernels for 0%

profile of v2, /device:TPU:0, one launch (start us, length us, event | category | flops | bytes accessed | tf_op | source)
XLA Modules:
  0.0 25.7 jit_solution(11481200515863327603)
XLA Ops:
  0.0 0.0 copy-start
  0.0 1.4 %copy-done = f32[1,2,768,256]{3,2,1,0:T(8,128)S(1)} copy-done((f32[1,2,768,256]{3,2,1,0:T(8,128)S(1)}, f32[1,2,768,256]{3,2,1,0:T(8,128)}, u32[]{:S(2)}) %copy-start) | copy-done | bytes 1572888
  1.4 0.0 copy-start.1
  1.4 1.1 %copy-done.1 = f32[1,2,768,128]{3,2,1,0:T(8,128)S(1)} copy-done((f32[1,2,768,128]{3,2,1,0:T(8,128)S(1)}, f32[1,2,768,128]{3,2,1,0:T(8,128)}, u32[]{:S(2)}) %copy-start.1) | copy-done | bytes 786456
  2.5 0.0 copy-start.2
  2.5 0.0 copy-start.3
  2.5 0.0 copy-start.4
  2.5 0.0 copy-start.5
  2.6 0.0 copy-start.6
  2.6 1.6 %project.1 = (f32[4,32,256]{2,1,0:T(8,128)S(1)}, f32[4,32,256]{2,1,0:T(8,128)S(1)}) custom-call(f32[1,2,768,256]{3,2,1,0:T(8,128)S(1)} %copy-done, f32[1,2,768,128]{3,2,1,0:T(8,128)S(1)} %copy-done.1), custom_call_target="tpu_custom_call" | custom-call | tf_op jit(solution)/shard_map/project/pallas_call | solution.py:76
  4.2 0.6 %collective-permute-start = (f32[4,32,256]{2,1,0:T(8,128)S(1)}, f32[4,32,256]{2,1,0:T(8,128)S(1)}, u32[]{:S(2)}, u32[]{:S(2)}) collective-permute-start(f32[4,32,256]{2,1,0:T(8,128)S(1)} %get-tuple-element.8), channel_id=1, source_target_pairs={{0,4},{4,0},{8,12},{12,8},{16,20},{20,16},{24,28},{28,24},{1,5},{5... | collective-permute-start | bytes 393224 | tf_op jit(solution)/shard_map/ppermute | solution.py:156
  4.8 1.0 %collective-permute-done = f32[4,32,256]{2,1,0:T(8,128)S(1)} collective-permute-done((f32[4,32,256]{2,1,0:T(8,128)S(1)}, f32[4,32,256]{2,1,0:T(8,128)S(1)}, u32[]{:S(2)}, u32[]{:S(2)}) %collective-permute-start) | collective-permute-done | bytes 131104 | tf_op jit(solution)/shard_map/ppermute | solution.py:156
  5.8 2.6 %collective-permute-start.1 = (f32[2,32,256]{2,1,0:T(8,128)S(1)}, f32[2,32,256]{2,1,0:T(8,128)S(1)}, u32[]{:S(2)}, u32[]{:S(2)}) collective-permute-start(f32[2,32,256]{2,1,0:T(8,128)S(1)} %pad_maximum_fusion), channel_id=1, source_target_pairs={{0,12},{4,8},{8,4},{12,0},{16,28},{20,24},{24,20},{28,16},{1,13},{... | collective-permute-start | bytes 196616 | tf_op jit(solution)/shard_map/ppermute | solution.py:156
  8.4 1.5 %collective-permute-start.2 = (f32[2,32,256]{2,1,0:T(8,128)S(1)}, f32[2,32,256]{2,1,0:T(8,128)S(1)}, u32[]{:S(2)}, u32[]{:S(2)}) collective-permute-start(f32[2,32,256]{2,1,0:T(8,128)S(1)} %pad_maximum_fusion.1), channel_id=1, source_target_pairs={{0,20},{4,16},{8,28},{12,24},{16,4},{20,0},{24,12},{28,8},{1,21},{... | collective-permute-start | bytes 196616 | tf_op jit(solution)/shard_map/ppermute | solution.py:156
  9.9 0.1 collective-permute-start.3
  10.0 0.7 %collective-permute-done.1.refs_2_ = f32[2,32,256]{2,1,0:T(8,128)S(1)} collective-permute-done((f32[2,32,256]{2,1,0:T(8,128)S(1)}, f32[2,32,256]{2,1,0:T(8,128)S(1)}, u32[]{:S(2)}, u32[]{:S(2)}) %collective-permute-start.1) | collective-permute-done | bytes 65568 | tf_op jit(solution)/shard_map/ppermute | solution.py:156
  10.7 1.6 %collective-permute-done.2.refs_3_ = f32[2,32,256]{2,1,0:T(8,128)S(1)} collective-permute-done((f32[2,32,256]{2,1,0:T(8,128)S(1)}, f32[2,32,256]{2,1,0:T(8,128)S(1)}, u32[]{:S(2)}, u32[]{:S(2)}) %collective-permute-start.2) | collective-permute-done | bytes 65568 | tf_op jit(solution)/shard_map/ppermute | solution.py:156
  12.3 2.8 %collective-permute-done.3.refs_4_ = f32[2,32,256]{2,1,0:T(8,128)S(1)} collective-permute-done((f32[2,32,256]{2,1,0:T(8,128)S(1)}, f32[2,32,256]{2,1,0:T(8,128)S(1)}, u32[]{:S(2)}, u32[]{:S(2)}) %collective-permute-start.3) | collective-permute-done | bytes 65568 | tf_op jit(solution)/shard_map/ppermute | solution.py:156
  15.1 0.0 copy-done.2
  15.1 0.0 copy-done.3
  15.1 0.0 copy-done.4
  15.1 0.0 copy-done.5
  15.1 0.0 copy-done.6
  15.1 0.8 %recombine.1.part_ref = f32[32,256]{1,0:T(8,128)S(1)} custom-call(f32[1,8]{1,0:T(1,128)S(1)} %bitcast.1, f32[1,2,4,256]{3,2,1,0:T(4,128)S(1)} %copy-done.2, f32[1,2,4,256]{3,2,1,0:T(4,128)S(1)} %copy-done.3, s32[1,4]{1,0:T(1,128)S(1)} %copy-done.5, s32[1,4]{1,0:T(1,128)S(1)} %copy-done.6, f32[1,32,256]{2,1,0:T(8,128)S(1)} %get-tuple-element.12.refs_0_, ...), custom_call_target="tpu_custom_call" | custom-call | tf_op jit(solution)/shard_map/recombine/pallas_call | solution.py:161
  16.0 3.7 %collective-permute-start.6 = (f32[32,256]{1,0:T(8,128)S(1)}, f32[32,256]{1,0:T(8,128)S(1)}, u32[]{:S(2)}, u32[]{:S(2)}) collective-permute-start(f32[32,256]{1,0:T(8,128)S(1)} %recombine.1.part_ref), channel_id=1, source_target_pairs={{0,3},{1,2},{2,1},{3,0},{4,7},{5,6},{6,5},{7,4},{8,11},{9,10},{10,... | collective-permute-start | bytes 98312 | tf_op jit(solution)/shard_map/ppermute | solution.py:156
  19.6 0.0 collective-permute-start.5
  19.6 0.8 %collective-permute-start.4 = (f32[32,256]{1,0:T(8,128)S(1)}, f32[32,256]{1,0:T(8,128)S(1)}, u32[]{:S(2)}, u32[]{:S(2)}) collective-permute-start(f32[32,256]{1,0:T(8,128)S(1)} %recombine.1.part_ref), channel_id=1, source_target_pairs={{0,1},{1,0},{2,3},{3,2},{4,5},{5,4},{6,7},{7,6},{8,9},{9,8},{10,11... | collective-permute-start | bytes 98312 | tf_op jit(solution)/shard_map/ppermute | solution.py:156
  20.4 1.3 %collective-permute-done.6.refs_2_ = f32[32,256]{1,0:T(8,128)S(1)} collective-permute-done((f32[32,256]{1,0:T(8,128)S(1)}, f32[32,256]{1,0:T(8,128)S(1)}, u32[]{:S(2)}, u32[]{:S(2)}) %collective-permute-start.6) | collective-permute-done | bytes 32800 | tf_op jit(solution)/shard_map/ppermute | solution.py:156
  21.7 2.7 %collective-permute-done.5.refs_1_ = f32[32,256]{1,0:T(8,128)S(1)} collective-permute-done((f32[32,256]{1,0:T(8,128)S(1)}, f32[32,256]{1,0:T(8,128)S(1)}, u32[]{:S(2)}, u32[]{:S(2)}) %collective-permute-start.5) | collective-permute-done | bytes 32800 | tf_op jit(solution)/shard_map/ppermute | solution.py:156
  24.4 0.0 collective-permute-done.4.refs_0_
  24.5 1.2 %smear.1 = f32[1,2,16,768]{3,2,1,0:T(8,128)} custom-call(f32[1,2,768,256]{3,2,1,0:T(8,128)S(1)} %copy-done, f32[32,256]{1,0:T(8,128)S(1)} %recombine.1.part_ref, f32[32,256]{1,0:T(8,128)S(1)} %collective-permute-done.4.refs_0_, f32[32,256]{1,0:T(8,128)S(1)} %collective-permute-done.5.refs_1_, f32[32,256]{1,0:T(8,128)S(1)} %collective-permute-done.6.refs_2_), custom_call_target="tpu_custom_call" | custom-call | tf_op jit(solution)/shard_map/smear/pallas_call | solution.py:180
  (5 shorter events, 0.0 us)
Async XLA Ops:
  0.0 1.4 %copy-start = (f32[1,2,768,256]{3,2,1,0:T(8,128)S(1)}, f32[1,2,768,256]{3,2,1,0:T(8,128)}, u32[]{:S(2)}) copy-start(f32[1,2,768,256]{3,2,1,0:T(8,128)} %evecs_ref.3) | copy-start | bytes 4718596
  1.4 1.1 %copy-start.1 = (f32[1,2,768,128]{3,2,1,0:T(8,128)S(1)}, f32[1,2,768,128]{3,2,1,0:T(8,128)}, u32[]{:S(2)}) copy-start(f32[1,2,768,128]{3,2,1,0:T(8,128)} %solutions_ref.1) | copy-start | bytes 2359300
  2.5 12.6 %copy-start.2 = (f32[1,2,4,256]{3,2,1,0:T(4,128)S(1)}, f32[1,2,4,256]{3,2,1,0:T(4,128)}, u32[]{:S(2)}) copy-start(f32[1,2,4,256]{3,2,1,0:T(4,128)} %noise_ref.1) | copy-start | bytes 24580
  2.5 12.6 %copy-start.3 = (f32[1,2,4,256]{3,2,1,0:T(4,128)S(1)}, f32[1,2,4,256]{3,2,1,0:T(4,128)}, u32[]{:S(2)}) copy-start(f32[1,2,4,256]{3,2,1,0:T(4,128)} %probe_ref.1) | copy-start | bytes 24580
  2.5 12.6 %copy-start.4 = (f32[8,1]{0,1:T(1,128)S(1)}, f32[8,1]{0,1:T(1,128)}, u32[]{:S(2)}) copy-start(f32[8,1]{0,1:T(1,128)} %param.9) | copy-start | bytes 100
  2.5 12.6 %copy-start.5 = (s32[1,4]{1,0:T(1,128)S(1)}, s32[1,4]{1,0:T(1,128)}, u32[]{:S(2)}) copy-start(s32[1,4]{1,0:T(1,128)} %spin_ref.1) | copy-start | bytes 52
  2.6 12.6 %copy-start.6 = (s32[1,4]{1,0:T(1,128)S(1)}, s32[1,4]{1,0:T(1,128)}, u32[]{:S(2)}) copy-start(s32[1,4]{1,0:T(1,128)} %lace_ref.1) | copy-start | bytes 52
  4.2 1.6 %collective-permute-start = (f32[4,32,256]{2,1,0:T(8,128)S(1)}, f32[4,32,256]{2,1,0:T(8,128)S(1)}, u32[]{:S(2)}, u32[]{:S(2)}) collective-permute-start(f32[4,32,256]{2,1,0:T(8,128)S(1)} %get-tuple-element.8), channel_id=1, source_target_pairs={{0,4},{4,0},{8,12},{12,8},{16,20},{20,16},{24,28},{28,24},{1,5},{5... | collective-permute-start | bytes 393224 | tf_op jit(solution)/shard_map/ppermute | solution.py:156
  5.8 4.9 %collective-permute-start.1 = (f32[2,32,256]{2,1,0:T(8,128)S(1)}, f32[2,32,256]{2,1,0:T(8,128)S(1)}, u32[]{:S(2)}, u32[]{:S(2)}) collective-permute-start(f32[2,32,256]{2,1,0:T(8,128)S(1)} %pad_maximum_fusion), channel_id=1, source_target_pairs={{0,12},{4,8},{8,4},{12,0},{16,28},{20,24},{24,20},{28,16},{1,13},{... | collective-permute-start | bytes 196616 | tf_op jit(solution)/shard_map/ppermute | solution.py:156
  8.4 3.9 %collective-permute-start.2 = (f32[2,32,256]{2,1,0:T(8,128)S(1)}, f32[2,32,256]{2,1,0:T(8,128)S(1)}, u32[]{:S(2)}, u32[]{:S(2)}) collective-permute-start(f32[2,32,256]{2,1,0:T(8,128)S(1)} %pad_maximum_fusion.1), channel_id=1, source_target_pairs={{0,20},{4,16},{8,28},{12,24},{16,4},{20,0},{24,12},{28,8},{1,21},{... | collective-permute-start | bytes 196616 | tf_op jit(solution)/shard_map/ppermute | solution.py:156
  9.9 5.2 %collective-permute-start.3 = (f32[2,32,256]{2,1,0:T(8,128)S(1)}, f32[2,32,256]{2,1,0:T(8,128)S(1)}, u32[]{:S(2)}, u32[]{:S(2)}) collective-permute-start(f32[2,32,256]{2,1,0:T(8,128)S(1)} %pad_maximum_fusion.2), channel_id=1, source_target_pairs={{0,24},{4,28},{8,16},{12,20},{16,8},{20,12},{24,0},{28,4},{1,25},{... | collective-permute-start | bytes 196616 | tf_op jit(solution)/shard_map/ppermute | solution.py:156
  16.0 5.8 %collective-permute-start.6 = (f32[32,256]{1,0:T(8,128)S(1)}, f32[32,256]{1,0:T(8,128)S(1)}, u32[]{:S(2)}, u32[]{:S(2)}) collective-permute-start(f32[32,256]{1,0:T(8,128)S(1)} %recombine.1.part_ref), channel_id=1, source_target_pairs={{0,3},{1,2},{2,1},{3,0},{4,7},{5,6},{6,5},{7,4},{8,11},{9,10},{10,... | collective-permute-start | bytes 98312 | tf_op jit(solution)/shard_map/ppermute | solution.py:156
  19.6 4.8 %collective-permute-start.5 = (f32[32,256]{1,0:T(8,128)S(1)}, f32[32,256]{1,0:T(8,128)S(1)}, u32[]{:S(2)}, u32[]{:S(2)}) collective-permute-start(f32[32,256]{1,0:T(8,128)S(1)} %recombine.1.part_ref), channel_id=1, source_target_pairs={{0,2},{1,3},{2,0},{3,1},{4,6},{5,7},{6,4},{7,5},{8,10},{9,11},{10,... | collective-permute-start | bytes 98312 | tf_op jit(solution)/shard_map/ppermute | solution.py:156
  19.6 4.8 %collective-permute-start.4 = (f32[32,256]{1,0:T(8,128)S(1)}, f32[32,256]{1,0:T(8,128)S(1)}, u32[]{:S(2)}, u32[]{:S(2)}) collective-permute-start(f32[32,256]{1,0:T(8,128)S(1)} %recombine.1.part_ref), channel_id=1, source_target_pairs={{0,1},{1,0},{2,3},{3,2},{4,5},{5,4},{6,7},{7,6},{8,9},{9,8},{10,11... | collective-permute-start | bytes 98312 | tf_op jit(solution)/shard_map/ppermute | solution.py:156

commit v3 on v2

v3 whole, which is shorter than its diff:
```python
import functools

import jax
import jax.numpy as jnp
from jax import lax
from jax.experimental import pallas as pl
from jax.experimental.pallas import tpu as pltpu
from jax.sharding import PartitionSpec as P

LACE_CLASSES = 8
STEP = 256
BF16 = jnp.bfloat16
F32 = jnp.float32
VMEM_SPEC = pl.BlockSpec(memory_space=pltpu.VMEM)
SMEM_SPEC = pl.BlockSpec(memory_space=pltpu.SMEM)


def split(x):
    high = x.astype(BF16)
    low = (x - high.astype(F32)).astype(BF16)
    return high, low


def dot3(left, right, contract=((1,), (0,))):
    lh, ll = left
    rh, rl = right
    mul = functools.partial(
        lax.dot_general, dimension_numbers=(contract, ((), ())), preferred_element_type=F32
    )
    rows = lh.shape[0]
    both = mul(jnp.concatenate([lh, ll], 0), rh)
    return both[:rows] + both[rows:] + mul(lh, rl)


def project_kernel(
    masks, evecs_hbm, solutions_hbm, keep_ref, send_ref, high_ref, low_ref, evecs_ref, solutions_ref, total_ref, sems
):
    chunks, _, step, modes = evecs_ref.shape
    cols = solutions_ref.shape[3]
    half = cols // (2 * len(masks))
    copies = []
    for i in range(chunks):
        rows = pl.ds(i * step, step)
        pair = (
            pltpu.make_async_copy(solutions_hbm.at[0, :, rows], solutions_ref.at[i], sems.at[0, i]),
            pltpu.make_async_copy(evecs_hbm.at[0, :, rows], evecs_ref.at[i], sems.at[1, i]),
        )
        for copy in pair:
            copy.start()
        copies.append(pair)
    for i in range(chunks):
        copies[i][0].wait()
        real = solutions_ref[i, 0].T
        imag = solutions_ref[i, 1].T
        left = split(
            jnp.concatenate(
                [jnp.concatenate([real, imag], 0), jnp.concatenate([imag, -real], 0)], 1
            )
        )
        copies[i][1].wait()
        right = split(evecs_ref[i].reshape(2 * step, modes))
        for ref, value in zip((high_ref, low_ref), right):
            for part in range(2):
                ref[part, i * step : (i + 1) * step] = value[part * step : (part + 1) * step]
        value = dot3(left, right)
        if i == 0:
            total_ref[...] = value
        else:
            total_ref[...] += value
    me = lax.axis_index("tm").astype(jnp.int32)
    for out, core in ((keep_ref, 1), (send_ref, 0)):
        for m, mask in enumerate(masks):
            block = me ^ (mask ^ core)
            for part in range(2):
                start = pl.multiple_of(part * cols + block * half, 8)
                out[m, part * half : (part + 1) * half] = total_ref[pl.ds(start, half)]


def project(evecs, solutions, masks):
    chips = len(masks)
    rows, modes = evecs.shape[2:]
    cols = solutions.shape[3]
    block_rows = 2 * cols // (2 * chips)
    step = STEP if rows % STEP == 0 else rows
    chunks = rows // step
    out = jax.ShapeDtypeStruct((chips, block_rows, modes), F32)
    held = jax.ShapeDtypeStruct((2, rows, modes), BF16)
    return pl.pallas_call(
        functools.partial(project_kernel, masks),
        in_specs=[pl.BlockSpec(memory_space=pltpu.HBM)] * 2,
        out_specs=[VMEM_SPEC] * 4,
        scratch_shapes=[
            pltpu.VMEM((chunks, 2, step, modes), F32),
            pltpu.VMEM((chunks, 2, step, cols), F32),
            pltpu.VMEM((2 * cols, modes), F32),
            pltpu.SemaphoreType.DMA((2, chunks)),
        ],
        out_shape=[out, out, held, held],
        compiler_params=pltpu.CompilerParams(vmem_limit_bytes=54_000_000),
        name="project",
    )(evecs, solutions)


def mixing_matrix(noise_ref, probe_ref, spin_ref, lace_ref, width):
    noise_real, noise_imag = noise_ref[0, 0], noise_ref[0, 1]
    probe_real, probe_imag = probe_ref[0, 0], probe_ref[0, 1]
    prod_real = noise_real * probe_real + noise_imag * probe_imag
    prod_imag = noise_real * probe_imag - noise_imag * probe_real
    spins, modes = prod_real.shape
    groups = width // spins
    prod = jnp.concatenate([prod_real] * groups + [prod_imag] * groups, 0)
    lanes = lax.broadcasted_iota(jnp.int32, (2 * width, modes), 1) % LACE_CLASSES
    row = lax.broadcasted_iota(jnp.int32, (2 * width, width), 0) % width
    col = lax.broadcasted_iota(jnp.int32, (2 * width, width), 1)
    same = (row // spins) == (col % groups)
    both = jnp.zeros((2 * width, width), F32)
    for k in range(width // groups):
        picked = jnp.sum(jnp.where(lanes == lace_ref[0, k], prod, 0.0), axis=1, keepdims=True)
        on = same & ((col // groups) == k) & ((row % spins) == spin_ref[0, k])
        both = both + jnp.where(on, picked, 0.0)
    real, imag = both[:width], both[width:]
    return jnp.concatenate(
        [jnp.concatenate([real, -imag], 1), jnp.concatenate([imag, real], 1)], 0
    )


def mix_kernel(noise_ref, probe_ref, spin_ref, lace_ref, out_ref):
    out_ref[...] = mixing_matrix(noise_ref, probe_ref, spin_ref, lace_ref, out_ref.shape[0] // 2)


def recombine_kernel(masks, weight_ref, keep_ref, recv_ref, *refs):
    others, out_ref = refs[:-1], refs[-1]
    me = lax.axis_index("tm").astype(jnp.int32)
    total = keep_ref[0] * weight_ref[0, me] + recv_ref[0] * weight_ref[0, me ^ 1]
    for mask, ref in zip(masks, others):
        total += ref[0] * weight_ref[0, me ^ mask] + ref[1] * weight_ref[0, me ^ mask ^ 1]
    out_ref[...] = total


def smear_kernel(high_ref, low_ref, mix_ref, *refs):
    out_ref = refs[-1]
    total = refs[0][...]
    for ref in refs[1:-1]:
        total += ref[...]
    total = dot3(split(mix_ref[...]), split(total))
    width = total.shape[0] // 2
    turned = jnp.concatenate([-total[width:], total[:width]], 0)
    across = ((1,), (1,))
    value = dot3(split(total), (high_ref[0], low_ref[0]), across)
    value += dot3(split(turned), (high_ref[1], low_ref[1]), across)
    out_ref[0, 0] = value[:width]
    out_ref[0, 1] = value[width:]


def per_device(
    evecs,
    solutions,
    sink_time_weight,
    noise_source_vector,
    probe,
    dilution_spin_index,
    dilution_lace_index,
):
    n_time, n_space = lax.axis_size("tm"), lax.axis_size("space")
    rows, modes = evecs.shape[2:]
    width = solutions.shape[3] // n_time
    chips = n_time // 2
    masks = [0] + [2 * m + 1 for m in range(1, chips)]
    keep, send, high, low = project(evecs, solutions, masks)

    def swap(value, mask, space=0):
        pairs = [
            (t * n_space + z, (t ^ mask) * n_space + (z ^ space))
            for t in range(n_time)
            for z in range(n_space)
        ]
        return lax.ppermute(value, ("tm", "space"), pairs)

    recv = swap(send, 1)
    weight = swap(sink_time_weight.T, 1)
    mix = pl.pallas_call(
        mix_kernel,
        in_specs=[VMEM_SPEC, VMEM_SPEC, SMEM_SPEC, SMEM_SPEC],
        out_specs=VMEM_SPEC,
        out_shape=jax.ShapeDtypeStruct((2 * width, 2 * width), F32),
        compiler_params=pltpu.CompilerParams(vmem_limit_bytes=8 << 20),
        name="mix",
    )(noise_source_vector, probe, dilution_spin_index, dilution_lace_index)
    pairs = [jnp.stack([keep[m], recv[m]]) for m in range(1, chips)]
    others = [swap(pair, mask) for pair, mask in zip(pairs, masks[1:])]
    part = pl.pallas_call(
        functools.partial(recombine_kernel, masks[1:]),
        in_specs=[SMEM_SPEC] + [VMEM_SPEC] * (chips + 1),
        out_specs=VMEM_SPEC,
        out_shape=jax.ShapeDtypeStruct((2 * width, modes), F32),
        compiler_params=pltpu.CompilerParams(vmem_limit_bytes=8 << 20),
        name="recombine",
    )(weight, keep[:1], recv[:1], *others)
    parts = [swap(part, 1, mask) for mask in reversed(range(n_space))]
    return pl.pallas_call(
        smear_kernel,
        in_specs=[VMEM_SPEC] * (n_space + 3),
        out_specs=VMEM_SPEC,
        out_shape=jax.ShapeDtypeStruct((1, 2, width, rows), F32),
        compiler_params=pltpu.CompilerParams(vmem_limit_bytes=16 << 20),
        name="smear",
    )(high, low, mix, *parts)


def solution(mesh):
    placed = (
        P("tm", None, "space", None),
        P("tm", None, "space", None),
        P(None, "tm"),
        P("tm", None, None, None),
        P("tm", None, None, None),
        P("tm", None),
        P("tm", None),
    )
    return jax.shard_map(
        per_device,
        mesh=mesh,
        in_specs=placed,
        out_specs=P("tm", None, None, "space"),
        check_vma=False,
    )
```

time: 25.9 us -> 22.5 us (0.87)
  waiting for transfers between devices: 10.1 us -> 7.39 us
  local copies, waits for them, and re-layouts: 2.58 us -> 0.04 us
  Pallas kernels: 3.7 us -> 5.6 us
    ppermute x7 -> x9, waiting for transfers between devices: 10.1 us -> 7.39 us  [swap(): return lax.ppermute(value, ('tm', 'space'), pairs)]
    unnamed x14 -> x10, local copies, waits for them, and re-layouts: 2.56 us -> 0.02 us
    pallas_call x2 -> x3, Pallas kernels: 2.86 us -> 5.03 us  [the longest x1 3.03 us: project(): pl.pallas_call(functools.partial(project_kernel, masks), in_specs=[pl.Blo...]
    pallas_call x1, Pallas kernels: 0.84 us -> 0.58 us  [per_device(): pl.pallas_call(functools.partial(recombine_kernel, masks[1:]), in_specs=[...]
    ppermute x7 -> x9, starting transfers between devices: 9.22 us -> 9.23 us  [swap(): return lax.ppermute(value, ('tm', 'space'), pairs)]
  transfers between devices with their start and end apart: 7 -> 9, of which waited for: 6 -> 7; matrix products, arithmetic and copies ran while one was open for 0% -> 0% of each run, Pallas kernels for 0% -> 3%
where the time goes in v3:
time: 22.5 us; the launch traced here: 22.3 us
  starting transfers between devices  9.23 us (41%)
  waiting for transfers between devices  7.39 us (33%)
  Pallas kernels  5.6 us (25%)
    ppermute x9, starting transfers between devices, swap(): return lax.ppermute(value, ('tm', 'space'), pairs)  9.23 us
    ppermute x9, waiting for transfers between devices, swap(): return lax.ppermute(value, ('tm', 'space'), pairs)  7.39 us
    pallas_call x1, Pallas kernels, project(): pl.pallas_call(functools.partial(project_kernel, masks), in_specs=[pl.Blo...  3.03 us
    pallas_call x1, Pallas kernels, per_device(): pl.pallas_call(smear_kernel, in_specs=[VMEM_SPEC] * (n_space + 3), out_sp...  1.29 us
    pallas_call x1, Pallas kernels, per_device(): pl.pallas_call(mix_kernel, in_specs=[VMEM_SPEC, VMEM_SPEC, SMEM_SPEC, SME...  0.71 us
    pallas_call x1, Pallas kernels, per_device(): pl.pallas_call(functools.partial(recombine_kernel, masks[1:]), in_specs=[...  0.58 us
  transfers between devices with their start and end apart: 9, of which 7 were waited for; matrix products, arithmetic and copies ran while one was open for 0% of the time, Pallas kernels for 3%

profile of v3, /device:TPU:0, one launch (start us, length us, event | category | flops | bytes accessed | tf_op | source)
XLA Modules:
  0.0 22.3 jit_solution(14726213985803906020)
XLA Ops:
  0.0 0.0 copy-start.4
  0.0 0.0 copy-start
  0.0 0.0 copy-start.1
  0.0 0.0 copy-start.2
  0.0 0.0 copy-start.3
  0.0 3.0 %project.1 = (f32[4,32,256]{2,1,0:T(8,128)S(1)}, f32[4,32,256]{2,1,0:T(8,128)S(1)}, bf16[2,768,256]{2,1,0:T(8,128)(2,1)S(1)}, bf16[2,768,256]{2,1,0:T(8,128)(2,1)S(1)}) custom-call(f32[1,2,768,256]{3,2,1,0:T(8,128)} %evecs_hbm.1, f32[1,2,768,128]{3,2,1,0:T(8,128)} %solutions_hbm.1), custom_call_target="tpu_custom_call" | custom-call | tf_op jit(solution)/shard_map/project/pallas_call | solution.py:88
  3.0 0.6 %collective-permute-start.1 = (f32[4,32,256]{2,1,0:T(8,128)S(1)}, f32[4,32,256]{2,1,0:T(8,128)S(1)}, u32[]{:S(2)}, u32[]{:S(2)}) collective-permute-start(f32[4,32,256]{2,1,0:T(8,128)S(1)} %get-tuple-element.12), channel_id=1, source_target_pairs={{0,4},{1,5},{2,6},{3,7},{4,0},{5,1},{6,2},{7,3},{8,12},{9,13},{10,... | collective-permute-start | bytes 393224 | tf_op jit(solution)/shard_map/ppermute | solution.py:177
  3.6 1.0 %collective-permute-done.1 = f32[4,32,256]{2,1,0:T(8,128)S(1)} collective-permute-done((f32[4,32,256]{2,1,0:T(8,128)S(1)}, f32[4,32,256]{2,1,0:T(8,128)S(1)}, u32[]{:S(2)}, u32[]{:S(2)}) %collective-permute-start.1) | collective-permute-done | bytes 131104 | tf_op jit(solution)/shard_map/ppermute | solution.py:177
  4.6 3.6 %collective-permute-start.4 = (f32[2,32,256]{2,1,0:T(8,128)S(1)}, f32[2,32,256]{2,1,0:T(8,128)S(1)}, u32[]{:S(2)}, u32[]{:S(2)}) collective-permute-start(f32[2,32,256]{2,1,0:T(8,128)S(1)} %pad_maximum_fusion.2), channel_id=1, source_target_pairs={{0,28},{1,29},{2,30},{3,31},{4,24},{5,25},{6,26},{7,27},{8,20},{9,... | collective-permute-start | bytes 196616 | tf_op jit(solution)/shard_map/ppermute | solution.py:177
  8.2 0.5 %collective-permute-start.3 = (f32[2,32,256]{2,1,0:T(8,128)S(1)}, f32[2,32,256]{2,1,0:T(8,128)S(1)}, u32[]{:S(2)}, u32[]{:S(2)}) collective-permute-start(f32[2,32,256]{2,1,0:T(8,128)S(1)} %pad_maximum_fusion.1), channel_id=1, source_target_pairs={{0,20},{1,21},{2,22},{3,23},{4,16},{5,17},{6,18},{7,19},{8,28},{9,... | collective-permute-start | bytes 196616 | tf_op jit(solution)/shard_map/ppermute | solution.py:177
  8.7 0.1 collective-permute-start.2
  8.9 0.0 copy-done.4
  8.9 0.1 collective-permute-start
  9.0 1.0 %collective-permute-done.weight_ref = f32[1,8]{1,0:T(1,128)S(1)} collective-permute-done((f32[1,8]{1,0:T(1,128)S(1)}, f32[1,8]{1,0:T(1,128)S(1)}, u32[]{:S(2)}, u32[]{:S(2)}) %collective-permute-start) | collective-permute-done | bytes 64 | tf_op jit(solution)/shard_map/ppermute | solution.py:177
  10.0 0.7 %collective-permute-done.4.refs_2_ = f32[2,32,256]{2,1,0:T(8,128)S(1)} collective-permute-done((f32[2,32,256]{2,1,0:T(8,128)S(1)}, f32[2,32,256]{2,1,0:T(8,128)S(1)}, u32[]{:S(2)}, u32[]{:S(2)}) %collective-permute-start.4) | collective-permute-done | bytes 65568 | tf_op jit(solution)/shard_map/ppermute | solution.py:177
  10.8 1.3 %collective-permute-done.3.refs_1_ = f32[2,32,256]{2,1,0:T(8,128)S(1)} collective-permute-done((f32[2,32,256]{2,1,0:T(8,128)S(1)}, f32[2,32,256]{2,1,0:T(8,128)S(1)}, u32[]{:S(2)}, u32[]{:S(2)}) %collective-permute-start.3) | collective-permute-done | bytes 65568 | tf_op jit(solution)/shard_map/ppermute | solution.py:177
  12.1 0.7 %collective-permute-done.2.refs_0_ = f32[2,32,256]{2,1,0:T(8,128)S(1)} collective-permute-done((f32[2,32,256]{2,1,0:T(8,128)S(1)}, f32[2,32,256]{2,1,0:T(8,128)S(1)}, u32[]{:S(2)}, u32[]{:S(2)}) %collective-permute-start.2) | collective-permute-done | bytes 65568 | tf_op jit(solution)/shard_map/ppermute | solution.py:177
  12.8 0.6 %recombine.1 = f32[32,256]{1,0:T(8,128)S(1)} custom-call(f32[1,8]{1,0:T(1,128)S(1)} %collective-permute-done.weight_ref, f32[1,32,256]{2,1,0:T(8,128)S(1)} %get-tuple-element.16.keep_ref, f32[1,32,256]{2,1,0:T(8,128)S(1)} %get-tuple-element.20.recv_ref, f32[2,32,256]{2,1,0:T(8,128)S(1)} %collective-permute-done.2.refs_0_, ...), custom_call_target="tpu_custom_call" | custom-call | tf_op jit(solution)/shard_map/recombine/pallas_call | solution.py:191
  13.4 3.4 %collective-permute-start.5 = (f32[32,256]{1,0:T(8,128)S(1)}, f32[32,256]{1,0:T(8,128)S(1)}, u32[]{:S(2)}, u32[]{:S(2)}) collective-permute-start(f32[32,256]{1,0:T(8,128)S(1)} %recombine.1), channel_id=1, source_target_pairs={{0,7},{1,6},{2,5},{3,4},{4,3},{5,2},{6,1},{7,0},{8,15},{9,14},{10,... | collective-permute-start | bytes 98312 | tf_op jit(solution)/shard_map/ppermute | solution.py:177
  16.8 0.0 collective-permute-start.6
  16.8 0.6 %collective-permute-start.7 = (f32[32,256]{1,0:T(8,128)S(1)}, f32[32,256]{1,0:T(8,128)S(1)}, u32[]{:S(2)}, u32[]{:S(2)}) collective-permute-start(f32[32,256]{1,0:T(8,128)S(1)} %recombine.1), channel_id=1, source_target_pairs={{0,5},{1,4},{2,7},{3,6},{4,1},{5,0},{6,3},{7,2},{8,13},{9,12},{10,... | collective-permute-start | bytes 98312 | tf_op jit(solution)/shard_map/ppermute | solution.py:177
  17.4 0.3 %collective-permute-start.8 = (f32[32,256]{1,0:T(8,128)S(1)}, f32[32,256]{1,0:T(8,128)S(1)}, u32[]{:S(2)}, u32[]{:S(2)}) collective-permute-start(f32[32,256]{1,0:T(8,128)S(1)} %recombine.1), channel_id=1, source_target_pairs={{0,4},{1,5},{2,6},{3,7},{4,0},{5,1},{6,2},{7,3},{8,12},{9,13},{10,... | collective-permute-start | bytes 98312 | tf_op jit(solution)/shard_map/ppermute | solution.py:177
  17.7 0.0 copy-done
  17.7 0.0 copy-done.1
  17.7 0.0 copy-done.2
  17.7 0.0 copy-done.3
  17.7 0.7 %mix.1.mix_ref = f32[32,32]{1,0:T(8,128)S(1)} custom-call(f32[1,2,4,256]{3,2,1,0:T(4,128)S(1)} %copy-done, f32[1,2,4,256]{3,2,1,0:T(4,128)S(1)} %copy-done.1, s32[1,4]{1,0:T(1,128)S(1)} %copy-done.2, s32[1,4]{1,0:T(1,128)S(1)} %copy-done.3), custom_call_target="tpu_custom_call" | custom-call | tf_op jit(solution)/shard_map/mix/pallas_call | solution.py:181
  18.4 0.2 collective-permute-done.5.refs_0_
  18.6 2.5 %collective-permute-done.6.refs_1_ = f32[32,256]{1,0:T(8,128)S(1)} collective-permute-done((f32[32,256]{1,0:T(8,128)S(1)}, f32[32,256]{1,0:T(8,128)S(1)}, u32[]{:S(2)}, u32[]{:S(2)}) %collective-permute-start.6) | collective-permute-done | bytes 32800 | tf_op jit(solution)/shard_map/ppermute | solution.py:177
  21.0 0.0 collective-permute-done.7.refs_2_
  21.0 0.0 collective-permute-done.8.refs_3_
  21.0 1.3 %smear.1 = f32[1,2,16,768]{3,2,1,0:T(8,128)} custom-call(bf16[2,768,256]{2,1,0:T(8,128)(2,1)S(1)} %get-tuple-element.9.high_ref, bf16[2,768,256]{2,1,0:T(8,128)(2,1)S(1)} %get-tuple-element.10.low_ref, f32[32,32]{1,0:T(8,128)S(1)} %mix.1.mix_ref, f32[32,256]{1,0:T(8,128)S(1)} %collective-permute-done.5.refs_0_, ...), custom_call_target="tpu_custom_call" | custom-call | tf_op jit(solution)/shard_map/smear/pallas_call | solution.py:200
  (5 shorter events, 0.0 us)
Async XLA Ops:
  0.0 8.9 %copy-start.4 = (f32[8,1]{0,1:T(1,128)S(1)}, f32[8,1]{0,1:T(1,128)}, u32[]{:S(2)}) copy-start(f32[8,1]{0,1:T(1,128)} %param.9) | copy-start | bytes 100
  0.0 17.6 %copy-start = (f32[1,2,4,256]{3,2,1,0:T(4,128)S(1)}, f32[1,2,4,256]{3,2,1,0:T(4,128)}, u32[]{:S(2)}) copy-start(f32[1,2,4,256]{3,2,1,0:T(4,128)} %noise_ref.1) | copy-start | bytes 24580
  0.0 17.7 %copy-start.1 = (f32[1,2,4,256]{3,2,1,0:T(4,128)S(1)}, f32[1,2,4,256]{3,2,1,0:T(4,128)}, u32[]{:S(2)}) copy-start(f32[1,2,4,256]{3,2,1,0:T(4,128)} %probe_ref.1) | copy-start | bytes 24580
  0.0 17.7 %copy-start.2 = (s32[1,4]{1,0:T(1,128)S(1)}, s32[1,4]{1,0:T(1,128)}, u32[]{:S(2)}) copy-start(s32[1,4]{1,0:T(1,128)} %spin_ref.1) | copy-start | bytes 52
  0.0 17.7 %copy-start.3 = (s32[1,4]{1,0:T(1,128)S(1)}, s32[1,4]{1,0:T(1,128)}, u32[]{:S(2)}) copy-start(s32[1,4]{1,0:T(1,128)} %lace_ref.1) | copy-start | bytes 52
  3.0 1.5 %collective-permute-start.1 = (f32[4,32,256]{2,1,0:T(8,128)S(1)}, f32[4,32,256]{2,1,0:T(8,128)S(1)}, u32[]{:S(2)}, u32[]{:S(2)}) collective-permute-start(f32[4,32,256]{2,1,0:T(8,128)S(1)} %get-tuple-element.12), channel_id=1, source_target_pairs={{0,4},{1,5},{2,6},{3,7},{4,0},{5,1},{6,2},{7,3},{8,12},{9,13},{10,... | collective-permute-start | bytes 393224 | tf_op jit(solution)/shard_map/ppermute | solution.py:177
  4.6 6.1 %collective-permute-start.4 = (f32[2,32,256]{2,1,0:T(8,128)S(1)}, f32[2,32,256]{2,1,0:T(8,128)S(1)}, u32[]{:S(2)}, u32[]{:S(2)}) collective-permute-start(f32[2,32,256]{2,1,0:T(8,128)S(1)} %pad_maximum_fusion.2), channel_id=1, source_target_pairs={{0,28},{1,29},{2,30},{3,31},{4,24},{5,25},{6,26},{7,27},{8,20},{9,... | collective-permute-start | bytes 196616 | tf_op jit(solution)/shard_map/ppermute | solution.py:177
  8.2 3.9 %collective-permute-start.3 = (f32[2,32,256]{2,1,0:T(8,128)S(1)}, f32[2,32,256]{2,1,0:T(8,128)S(1)}, u32[]{:S(2)}, u32[]{:S(2)}) collective-permute-start(f32[2,32,256]{2,1,0:T(8,128)S(1)} %pad_maximum_fusion.1), channel_id=1, source_target_pairs={{0,20},{1,21},{2,22},{3,23},{4,16},{5,17},{6,18},{7,19},{8,28},{9,... | collective-permute-start | bytes 196616 | tf_op jit(solution)/shard_map/ppermute | solution.py:177
  8.7 4.1 %collective-permute-start.2 = (f32[2,32,256]{2,1,0:T(8,128)S(1)}, f32[2,32,256]{2,1,0:T(8,128)S(1)}, u32[]{:S(2)}, u32[]{:S(2)}) collective-permute-start(f32[2,32,256]{2,1,0:T(8,128)S(1)} %pad_maximum_fusion), channel_id=1, source_target_pairs={{0,12},{1,13},{2,14},{3,15},{4,8},{5,9},{6,10},{7,11},{8,4},{9,5},... | collective-permute-start | bytes 196616 | tf_op jit(solution)/shard_map/ppermute | solution.py:177
  8.9 1.2 %collective-permute-start = (f32[1,8]{1,0:T(1,128)S(1)}, f32[1,8]{1,0:T(1,128)S(1)}, u32[]{:S(2)}, u32[]{:S(2)}) collective-permute-start(f32[1,8]{1,0:T(1,128)S(1)} %bitcast.1), channel_id=1, source_target_pairs={{0,4},{1,5},{2,6},{3,7},{4,0},{5,1},{6,2},{7,3},{8,12},{9,13},{10,... | collective-permute-start | bytes 104 | tf_op jit(solution)/shard_map/ppermute | solution.py:177
  13.4 5.2 %collective-permute-start.5 = (f32[32,256]{1,0:T(8,128)S(1)}, f32[32,256]{1,0:T(8,128)S(1)}, u32[]{:S(2)}, u32[]{:S(2)}) collective-permute-start(f32[32,256]{1,0:T(8,128)S(1)} %recombine.1), channel_id=1, source_target_pairs={{0,7},{1,6},{2,5},{3,4},{4,3},{5,2},{6,1},{7,0},{8,15},{9,14},{10,... | collective-permute-start | bytes 98312 | tf_op jit(solution)/shard_map/ppermute | solution.py:177
  16.8 4.2 %collective-permute-start.6 = (f32[32,256]{1,0:T(8,128)S(1)}, f32[32,256]{1,0:T(8,128)S(1)}, u32[]{:S(2)}, u32[]{:S(2)}) collective-permute-start(f32[32,256]{1,0:T(8,128)S(1)} %recombine.1), channel_id=1, source_target_pairs={{0,6},{1,7},{2,4},{3,5},{4,2},{5,3},{6,0},{7,1},{8,14},{9,15},{10,... | collective-permute-start | bytes 98312 | tf_op jit(solution)/shard_map/ppermute | solution.py:177
  16.8 4.2 %collective-permute-start.7 = (f32[32,256]{1,0:T(8,128)S(1)}, f32[32,256]{1,0:T(8,128)S(1)}, u32[]{:S(2)}, u32[]{:S(2)}) collective-permute-start(f32[32,256]{1,0:T(8,128)S(1)} %recombine.1), channel_id=1, source_target_pairs={{0,5},{1,4},{2,7},{3,6},{4,1},{5,0},{6,3},{7,2},{8,13},{9,12},{10,... | collective-permute-start | bytes 98312 | tf_op jit(solution)/shard_map/ppermute | solution.py:177
  17.4 3.6 %collective-permute-start.8 = (f32[32,256]{1,0:T(8,128)S(1)}, f32[32,256]{1,0:T(8,128)S(1)}, u32[]{:S(2)}, u32[]{:S(2)}) collective-permute-start(f32[32,256]{1,0:T(8,128)S(1)} %recombine.1), channel_id=1, source_target_pairs={{0,4},{1,5},{2,6},{3,7},{4,0},{5,1},{6,2},{7,3},{8,12},{9,13},{10,... | collective-permute-start | bytes 98312 | tf_op jit(solution)/shard_map/ppermute | solution.py:177

commit v4 on v3

--- a/solution.py
+++ b/solution.py
@@ -8,7 +8,7 @@
 from jax.sharding import PartitionSpec as P
 
 LACE_CLASSES = 8
-STEP = 256
+STEP = 384
 BF16 = jnp.bfloat16
 F32 = jnp.float32
 VMEM_SPEC = pl.BlockSpec(memory_space=pltpu.VMEM)
@@ -124,17 +124,28 @@
     )
 
 
-def mix_kernel(noise_ref, probe_ref, spin_ref, lace_ref, out_ref):
+def mix_kernel(masks, noise_ref, probe_ref, spin_ref, lace_ref, weight_ref, out_ref, rows_ref):
+    partner = lax.axis_index("tm").astype(jnp.int32) ^ 1
+    for i, mask in enumerate(masks):
+        for core in range(2):
+            value = weight_ref[0, partner ^ mask ^ core]
+            rows_ref[2 * i + core : 2 * i + core + 1] = jnp.full((1, rows_ref.shape[1]), value)
     out_ref[...] = mixing_matrix(noise_ref, probe_ref, spin_ref, lace_ref, out_ref.shape[0] // 2)
 
 
-def recombine_kernel(masks, weight_ref, keep_ref, recv_ref, *refs):
+def recombine_kernel(weight_ref, keep_ref, recv_ref, *refs):
     others, out_ref = refs[:-1], refs[-1]
-    me = lax.axis_index("tm").astype(jnp.int32)
-    total = keep_ref[0] * weight_ref[0, me] + recv_ref[0] * weight_ref[0, me ^ 1]
-    for mask, ref in zip(masks, others):
-        total += ref[0] * weight_ref[0, me ^ mask] + ref[1] * weight_ref[0, me ^ mask ^ 1]
+    total = keep_ref[0] * weight_ref[0:1] + recv_ref[0] * weight_ref[1:2]
+    for i, ref in enumerate(others):
+        total += ref[0] * weight_ref[2 * i + 2 : 2 * i + 3]
+        total += ref[1] * weight_ref[2 * i + 3 : 2 * i + 4]
     out_ref[...] = total
+
+
+def turn_kernel(high_ref, low_ref, high_out, low_out):
+    for part in range(2):
+        high_out[part] = high_ref[part].T
+        low_out[part] = low_ref[part].T
 
 
 def smear_kernel(high_ref, low_ref, mix_ref, *refs):
@@ -145,7 +156,7 @@
     total = dot3(split(mix_ref[...]), split(total))
     width = total.shape[0] // 2
     turned = jnp.concatenate([-total[width:], total[:width]], 0)
-    across = ((1,), (1,))
+    across = ((1,), (0,))
     value = dot3(split(total), (high_ref[0], low_ref[0]), across)
     value += dot3(split(turned), (high_ref[1], low_ref[1]), across)
     out_ref[0, 0] = value[:width]
@@ -177,20 +188,32 @@
         return lax.ppermute(value, ("tm", "space"), pairs)
 
     recv = swap(send, 1)
-    weight = swap(sink_time_weight.T, 1)
-    mix = pl.pallas_call(
-        mix_kernel,
-        in_specs=[VMEM_SPEC, VMEM_SPEC, SMEM_SPEC, SMEM_SPEC],
-        out_specs=VMEM_SPEC,
-        out_shape=jax.ShapeDtypeStruct((2 * width, 2 * width), F32),
+    mix, weight = pl.pallas_call(
+        functools.partial(mix_kernel, masks),
+        in_specs=[VMEM_SPEC, VMEM_SPEC, SMEM_SPEC, SMEM_SPEC, SMEM_SPEC],
+        out_specs=[VMEM_SPEC, VMEM_SPEC],
+        out_shape=[
+            jax.ShapeDtypeStruct((2 * width, 2 * width), F32),
+            jax.ShapeDtypeStruct((n_time, modes), F32),
+        ],
         compiler_params=pltpu.CompilerParams(vmem_limit_bytes=8 << 20),
         name="mix",
-    )(noise_source_vector, probe, dilution_spin_index, dilution_lace_index)
+    )(noise_source_vector, probe, dilution_spin_index, dilution_lace_index, sink_time_weight.T)
+    weight = swap(weight, 1)
+    turned = jax.ShapeDtypeStruct((2, modes, rows), BF16)
+    high, low = pl.pallas_call(
+        turn_kernel,
+        in_specs=[VMEM_SPEC, VMEM_SPEC],
+        out_specs=[VMEM_SPEC, VMEM_SPEC],
+        out_shape=[turned, turned],
+        compiler_params=pltpu.CompilerParams(vmem_limit_bytes=8 << 20),
+        name="turn",
+    )(high, low)
     pairs = [jnp.stack([keep[m], recv[m]]) for m in range(1, chips)]
     others = [swap(pair, mask) for pair, mask in zip(pairs, masks[1:])]
     part = pl.pallas_call(
-        functools.partial(recombine_kernel, masks[1:]),
-        in_specs=[SMEM_SPEC] + [VMEM_SPEC] * (chips + 1),
+        recombine_kernel,
+        in_specs=[VMEM_SPEC] * (chips + 2),
         out_specs=VMEM_SPEC,
         out_shape=jax.ShapeDtypeStruct((2 * width, modes), F32),
         compiler_params=pltpu.CompilerParams(vmem_limit_bytes=8 << 20),

time: 22.5 us -> 21.5 us (0.956)
  Pallas kernels: 5.6 us -> 5.11 us
  waiting for transfers between devices: 7.39 us -> 6.91 us
    ppermute x9, waiting for transfers between devices: 7.39 us -> 6.91 us  [swap(): return lax.ppermute(value, ('tm', 'space'), pairs)]
    pallas_call x1, Pallas kernels: 3.03 us -> 2.8 us  [project(): pl.pallas_call(functools.partial(project_kernel, masks), in_specs=[pl.Blo...]
    pallas_call x2 -> x3, Pallas kernels: 1.28 us -> 1.19 us  [the longest x1 0.71 us: per_device(): pl.pallas_call(functools.partial(mix_kernel, masks), in_specs=[VMEM_SPEC,...]
  transfers between devices with their start and end apart: 9 -> 9, of which waited for: 7 -> 6; matrix products, arithmetic and copies ran while one was open for 0% -> 0% of each run, Pallas kernels for 3% -> 5%
where the time goes in v4:
time: 21.5 us; the launch traced here: 21.4 us
  starting transfers between devices  9.23 us (43%)
  waiting for transfers between devices  6.91 us (32%)
  Pallas kernels  5.11 us (24%)
    ppermute x9, starting transfers between devices, swap(): return lax.ppermute(value, ('tm', 'space'), pairs)  9.23 us
    ppermute x9, waiting for transfers between devices, swap(): return lax.ppermute(value, ('tm', 'space'), pairs)  6.91 us
    pallas_call x1, Pallas kernels, project(): pl.pallas_call(functools.partial(project_kernel, masks), in_specs=[pl.Blo...  2.8 us
    pallas_call x1, Pallas kernels, per_device(): pl.pallas_call(smear_kernel, in_specs=[VMEM_SPEC] * (n_space + 3), out_sp...  1.12 us
    pallas_call x1, Pallas kernels, per_device(): pl.pallas_call(functools.partial(mix_kernel, masks), in_specs=[VMEM_SPEC,...  0.71 us
    pallas_call x1, Pallas kernels, per_device(): pl.pallas_call(turn_kernel, in_specs=[VMEM_SPEC, VMEM_SPEC], out_specs=[V...  0.45 us
  transfers between devices with their start and end apart: 9, of which 6 were waited for; matrix products, arithmetic and copies ran while one was open for 0% of the time, Pallas kernels for 5%

profile of v4, /device:TPU:0, one launch (start us, length us, event | category | flops | bytes accessed | tf_op | source)
XLA Modules:
  0.0 21.4 jit_solution(3713440131319648288)
XLA Ops:
  0.0 0.0 copy-start.4
  0.0 0.0 copy-start
  0.0 0.0 copy-start.1
  0.0 0.0 copy-start.2
  0.0 0.0 copy-start.3
  0.0 2.8 %project.1 = (f32[4,32,256]{2,1,0:T(8,128)S(1)}, f32[4,32,256]{2,1,0:T(8,128)S(1)}, bf16[2,768,256]{2,1,0:T(8,128)(2,1)S(1)}, bf16[2,768,256]{2,1,0:T(8,128)(2,1)S(1)}) custom-call(f32[1,2,768,256]{3,2,1,0:T(8,128)} %evecs_hbm.1, f32[1,2,768,128]{3,2,1,0:T(8,128)} %solutions_hbm.1), custom_call_target="tpu_custom_call" | custom-call | tf_op jit(solution)/shard_map/project/pallas_call | solution.py:88
  2.8 0.6 %collective-permute-start.1 = (f32[4,32,256]{2,1,0:T(8,128)S(1)}, f32[4,32,256]{2,1,0:T(8,128)S(1)}, u32[]{:S(2)}, u32[]{:S(2)}) collective-permute-start(f32[4,32,256]{2,1,0:T(8,128)S(1)} %get-tuple-element.20), channel_id=1, source_target_pairs={{0,4},{1,5},{2,6},{3,7},{4,0},{5,1},{6,2},{7,3},{8,12},{9,13},{10,... | collective-permute-start | bytes 393224 | tf_op jit(solution)/shard_map/ppermute | solution.py:188
  3.4 1.0 %collective-permute-done.1 = f32[4,32,256]{2,1,0:T(8,128)S(1)} collective-permute-done((f32[4,32,256]{2,1,0:T(8,128)S(1)}, f32[4,32,256]{2,1,0:T(8,128)S(1)}, u32[]{:S(2)}, u32[]{:S(2)}) %collective-permute-start.1) | collective-permute-done | bytes 131104 | tf_op jit(solution)/shard_map/ppermute | solution.py:188
  4.4 3.6 %collective-permute-start.4 = (f32[2,32,256]{2,1,0:T(8,128)S(1)}, f32[2,32,256]{2,1,0:T(8,128)S(1)}, u32[]{:S(2)}, u32[]{:S(2)}) collective-permute-start(f32[2,32,256]{2,1,0:T(8,128)S(1)} %pad_maximum_fusion.2), channel_id=1, source_target_pairs={{0,28},{1,29},{2,30},{3,31},{4,24},{5,25},{6,26},{7,27},{8,20},{9,... | collective-permute-start | bytes 196616 | tf_op jit(solution)/shard_map/ppermute | solution.py:188
  8.0 0.5 %collective-permute-start.3 = (f32[2,32,256]{2,1,0:T(8,128)S(1)}, f32[2,32,256]{2,1,0:T(8,128)S(1)}, u32[]{:S(2)}, u32[]{:S(2)}) collective-permute-start(f32[2,32,256]{2,1,0:T(8,128)S(1)} %pad_maximum_fusion.1), channel_id=1, source_target_pairs={{0,20},{1,21},{2,22},{3,23},{4,16},{5,17},{6,18},{7,19},{8,28},{9,... | collective-permute-start | bytes 196616 | tf_op jit(solution)/shard_map/ppermute | solution.py:188
  8.5 0.1 collective-permute-start.2
  8.6 0.0 copy-done.4
  8.6 0.0 copy-done
  8.6 0.0 copy-done.1
  8.6 0.0 copy-done.2
  8.7 0.0 copy-done.3
  8.7 0.7 %mix.1 = (f32[32,32]{1,0:T(8,128)S(1)}, f32[8,256]{1,0:T(8,128)S(1)}) custom-call(f32[1,2,4,256]{3,2,1,0:T(4,128)S(1)} %copy-done, f32[1,2,4,256]{3,2,1,0:T(4,128)S(1)} %copy-done.1, s32[1,4]{1,0:T(1,128)S(1)} %copy-done.2, s32[1,4]{1,0:T(1,128)S(1)} %copy-done.3, f32[1,8]{1,0:T(1,128)S(1)} %bitcast.1), custom_call_target="tpu_custom_call" | custom-call | tf_op jit(solution)/shard_map/mix/pallas_call | solution.py:191
  9.4 0.2 collective-permute-start
  9.5 1.0 %collective-permute-done.weight_ref = f32[8,256]{1,0:T(8,128)S(1)} collective-permute-done((f32[8,256]{1,0:T(8,128)S(1)}, f32[8,256]{1,0:T(8,128)S(1)}, u32[]{:S(2)}, u32[]{:S(2)}) %collective-permute-start) | collective-permute-done | bytes 8224 | tf_op jit(solution)/shard_map/ppermute | solution.py:188
  10.6 0.0 collective-permute-done.4.refs_2_
  10.6 1.3 %collective-permute-done.3.refs_1_ = f32[2,32,256]{2,1,0:T(8,128)S(1)} collective-permute-done((f32[2,32,256]{2,1,0:T(8,128)S(1)}, f32[2,32,256]{2,1,0:T(8,128)S(1)}, u32[]{:S(2)}, u32[]{:S(2)}) %collective-permute-start.3) | collective-permute-done | bytes 65568 | tf_op jit(solution)/shard_map/ppermute | solution.py:188
  11.9 0.7 %collective-permute-done.2.refs_0_ = f32[2,32,256]{2,1,0:T(8,128)S(1)} collective-permute-done((f32[2,32,256]{2,1,0:T(8,128)S(1)}, f32[2,32,256]{2,1,0:T(8,128)S(1)}, u32[]{:S(2)}, u32[]{:S(2)}) %collective-permute-start.2) | collective-permute-done | bytes 65568 | tf_op jit(solution)/shard_map/ppermute | solution.py:188
  12.6 3.4 %collective-permute-start.5 = (f32[32,256]{1,0:T(8,128)S(1)}, f32[32,256]{1,0:T(8,128)S(1)}, u32[]{:S(2)}, u32[]{:S(2)}) collective-permute-start(f32[32,256]{1,0:T(8,128)S(1)} %recombine.1), channel_id=1, source_target_pairs={{0,7},{1,6},{2,5},{3,4},{4,3},{5,2},{6,1},{7,0},{8,15},{9,14},{10,... | collective-permute-start | bytes 98312 | tf_op jit(solution)/shard_map/ppermute | solution.py:188
  16.0 0.0 collective-permute-start.6
  16.0 0.6 %collective-permute-start.7 = (f32[32,256]{1,0:T(8,128)S(1)}, f32[32,256]{1,0:T(8,128)S(1)}, u32[]{:S(2)}, u32[]{:S(2)}) collective-permute-start(f32[32,256]{1,0:T(8,128)S(1)} %recombine.1), channel_id=1, source_target_pairs={{0,5},{1,4},{2,7},{3,6},{4,1},{5,0},{6,3},{7,2},{8,13},{9,12},{10,... | collective-permute-start | bytes 98312 | tf_op jit(solution)/shard_map/ppermute | solution.py:188
  16.6 0.3 %collective-permute-start.8 = (f32[32,256]{1,0:T(8,128)S(1)}, f32[32,256]{1,0:T(8,128)S(1)}, u32[]{:S(2)}, u32[]{:S(2)}) collective-permute-start(f32[32,256]{1,0:T(8,128)S(1)} %recombine.1), channel_id=1, source_target_pairs={{0,4},{1,5},{2,6},{3,7},{4,0},{5,1},{6,2},{7,3},{8,12},{9,13},{10,... | collective-permute-start | bytes 98312 | tf_op jit(solution)/shard_map/ppermute | solution.py:188
  16.9 0.5 %turn.1 = (bf16[2,256,768]{2,1,0:T(8,128)(2,1)S(1)}, bf16[2,256,768]{2,1,0:T(8,128)(2,1)S(1)}) custom-call(bf16[2,768,256]{2,1,0:T(8,128)(2,1)S(1)} %get-tuple-element.13.high_ref, bf16[2,768,256]{2,1,0:T(8,128)(2,1)S(1)} %get-tuple-element.14.low_ref), custom_call_target="tpu_custom_call" | custom-call | tf_op jit(solution)/shard_map/turn/pallas_call | solution.py:204
  17.3 0.5 %collective-permute-done.5.refs_0_ = f32[32,256]{1,0:T(8,128)S(1)} collective-permute-done((f32[32,256]{1,0:T(8,128)S(1)}, f32[32,256]{1,0:T(8,128)S(1)}, u32[]{:S(2)}, u32[]{:S(2)}) %collective-permute-start.5) | collective-permute-done | bytes 32800 | tf_op jit(solution)/shard_map/ppermute | solution.py:188
  17.8 2.5 %collective-permute-done.6.refs_1_ = f32[32,256]{1,0:T(8,128)S(1)} collective-permute-done((f32[32,256]{1,0:T(8,128)S(1)}, f32[32,256]{1,0:T(8,128)S(1)}, u32[]{:S(2)}, u32[]{:S(2)}) %collective-permute-start.6) | collective-permute-done | bytes 32800 | tf_op jit(solution)/shard_map/ppermute | solution.py:188
  20.2 0.0 collective-permute-done.7.refs_2_
  20.2 0.0 collective-permute-done.8.refs_3_
  20.3 1.1 %smear.1 = f32[1,2,16,768]{3,2,1,0:T(8,128)} custom-call(bf16[2,256,768]{2,1,0:T(8,128)(2,1)S(1)} %get-tuple-element.15.high_ref, bf16[2,256,768]{2,1,0:T(8,128)(2,1)S(1)} %get-tuple-element.16.low_ref, f32[32,32]{1,0:T(8,128)S(1)} %get-tuple-element.17.mix_ref, f32[32,256]{1,0:T(8,128)S(1)} %collective-permute-done.5.refs_0_, ...), custom_call_target="tpu_custom_call" | custom-call | tf_op jit(solution)/shard_map/smear/pallas_call | solution.py:223
  (6 shorter events, 0.1 us)
Async XLA Ops:
  0.0 8.6 %copy-start.4 = (f32[8,1]{0,1:T(1,128)S(1)}, f32[8,1]{0,1:T(1,128)}, u32[]{:S(2)}) copy-start(f32[8,1]{0,1:T(1,128)} %param.9) | copy-start | bytes 100
  0.0 8.6 %copy-start = (f32[1,2,4,256]{3,2,1,0:T(4,128)S(1)}, f32[1,2,4,256]{3,2,1,0:T(4,128)}, u32[]{:S(2)}) copy-start(f32[1,2,4,256]{3,2,1,0:T(4,128)} %noise_ref.1) | copy-start | bytes 24580
  0.0 8.6 %copy-start.1 = (f32[1,2,4,256]{3,2,1,0:T(4,128)S(1)}, f32[1,2,4,256]{3,2,1,0:T(4,128)}, u32[]{:S(2)}) copy-start(f32[1,2,4,256]{3,2,1,0:T(4,128)} %probe_ref.1) | copy-start | bytes 24580
  0.0 8.6 %copy-start.2 = (s32[1,4]{1,0:T(1,128)S(1)}, s32[1,4]{1,0:T(1,128)}, u32[]{:S(2)}) copy-start(s32[1,4]{1,0:T(1,128)} %spin_ref.1) | copy-start | bytes 52
  0.0 8.6 %copy-start.3 = (s32[1,4]{1,0:T(1,128)S(1)}, s32[1,4]{1,0:T(1,128)}, u32[]{:S(2)}) copy-start(s32[1,4]{1,0:T(1,128)} %lace_ref.1) | copy-start | bytes 52
  2.8 1.5 %collective-permute-start.1 = (f32[4,32,256]{2,1,0:T(8,128)S(1)}, f32[4,32,256]{2,1,0:T(8,128)S(1)}, u32[]{:S(2)}, u32[]{:S(2)}) collective-permute-start(f32[4,32,256]{2,1,0:T(8,128)S(1)} %get-tuple-element.20), channel_id=1, source_target_pairs={{0,4},{1,5},{2,6},{3,7},{4,0},{5,1},{6,2},{7,3},{8,12},{9,13},{10,... | collective-permute-start | bytes 393224 | tf_op jit(solution)/shard_map/ppermute | solution.py:188
  4.4 6.2 %collective-permute-start.4 = (f32[2,32,256]{2,1,0:T(8,128)S(1)}, f32[2,32,256]{2,1,0:T(8,128)S(1)}, u32[]{:S(2)}, u32[]{:S(2)}) collective-permute-start(f32[2,32,256]{2,1,0:T(8,128)S(1)} %pad_maximum_fusion.2), channel_id=1, source_target_pairs={{0,28},{1,29},{2,30},{3,31},{4,24},{5,25},{6,26},{7,27},{8,20},{9,... | collective-permute-start | bytes 196616 | tf_op jit(solution)/shard_map/ppermute | solution.py:188
  8.0 3.9 %collective-permute-start.3 = (f32[2,32,256]{2,1,0:T(8,128)S(1)}, f32[2,32,256]{2,1,0:T(8,128)S(1)}, u32[]{:S(2)}, u32[]{:S(2)}) collective-permute-start(f32[2,32,256]{2,1,0:T(8,128)S(1)} %pad_maximum_fusion.1), channel_id=1, source_target_pairs={{0,20},{1,21},{2,22},{3,23},{4,16},{5,17},{6,18},{7,19},{8,28},{9,... | collective-permute-start | bytes 196616 | tf_op jit(solution)/shard_map/ppermute | solution.py:188
  8.5 4.1 %collective-permute-start.2 = (f32[2,32,256]{2,1,0:T(8,128)S(1)}, f32[2,32,256]{2,1,0:T(8,128)S(1)}, u32[]{:S(2)}, u32[]{:S(2)}) collective-permute-start(f32[2,32,256]{2,1,0:T(8,128)S(1)} %pad_maximum_fusion), channel_id=1, source_target_pairs={{0,12},{1,13},{2,14},{3,15},{4,8},{5,9},{6,10},{7,11},{8,4},{9,5},... | collective-permute-start | bytes 196616 | tf_op jit(solution)/shard_map/ppermute | solution.py:188
  9.4 1.2 %collective-permute-start = (f32[8,256]{1,0:T(8,128)S(1)}, f32[8,256]{1,0:T(8,128)S(1)}, u32[]{:S(2)}, u32[]{:S(2)}) collective-permute-start(f32[8,256]{1,0:T(8,128)S(1)} %get-tuple-element.18), channel_id=1, source_target_pairs={{0,4},{1,5},{2,6},{3,7},{4,0},{5,1},{6,2},{7,3},{8,12},{9,13},{10,... | collective-permute-start | bytes 24584 | tf_op jit(solution)/shard_map/ppermute | solution.py:188
  12.6 5.2 %collective-permute-start.5 = (f32[32,256]{1,0:T(8,128)S(1)}, f32[32,256]{1,0:T(8,128)S(1)}, u32[]{:S(2)}, u32[]{:S(2)}) collective-permute-start(f32[32,256]{1,0:T(8,128)S(1)} %recombine.1), channel_id=1, source_target_pairs={{0,7},{1,6},{2,5},{3,4},{4,3},{5,2},{6,1},{7,0},{8,15},{9,14},{10,... | collective-permute-start | bytes 98312 | tf_op jit(solution)/shard_map/ppermute | solution.py:188
  16.0 4.2 %collective-permute-start.6 = (f32[32,256]{1,0:T(8,128)S(1)}, f32[32,256]{1,0:T(8,128)S(1)}, u32[]{:S(2)}, u32[]{:S(2)}) collective-permute-start(f32[32,256]{1,0:T(8,128)S(1)} %recombine.1), channel_id=1, source_target_pairs={{0,6},{1,7},{2,4},{3,5},{4,2},{5,3},{6,0},{7,1},{8,14},{9,15},{10,... | collective-permute-start | bytes 98312 | tf_op jit(solution)/shard_map/ppermute | solution.py:188
  16.0 4.2 %collective-permute-start.7 = (f32[32,256]{1,0:T(8,128)S(1)}, f32[32,256]{1,0:T(8,128)S(1)}, u32[]{:S(2)}, u32[]{:S(2)}) collective-permute-start(f32[32,256]{1,0:T(8,128)S(1)} %recombine.1), channel_id=1, source_target_pairs={{0,5},{1,4},{2,7},{3,6},{4,1},{5,0},{6,3},{7,2},{8,13},{9,12},{10,... | collective-permute-start | bytes 98312 | tf_op jit(solution)/shard_map/ppermute | solution.py:188
  16.6 3.6 %collective-permute-start.8 = (f32[32,256]{1,0:T(8,128)S(1)}, f32[32,256]{1,0:T(8,128)S(1)}, u32[]{:S(2)}, u32[]{:S(2)}) collective-permute-start(f32[32,256]{1,0:T(8,128)S(1)} %recombine.1), channel_id=1, source_target_pairs={{0,4},{1,5},{2,6},{3,7},{4,0},{5,1},{6,2},{7,3},{8,12},{9,13},{10,... | collective-permute-start | bytes 98312 | tf_op jit(solution)/shard_map/ppermute | solution.py:188

commit v5 on v4

--- a/solution.py
+++ b/solution.py
@@ -33,7 +33,8 @@
 
 
 def project_kernel(
-    masks, evecs_hbm, solutions_hbm, keep_ref, send_ref, high_ref, low_ref, evecs_ref, solutions_ref, total_ref, sems
+    masks, evecs_hbm, solutions_hbm, send_ref, high_ref, low_ref, keep_high_ref, keep_low_ref,
+    evecs_ref, solutions_ref, turned_ref, sems
 ):
     chunks, _, step, modes = evecs_ref.shape
     cols = solutions_ref.shape[3]
@@ -48,32 +49,39 @@
         for copy in pair:
             copy.start()
         copies.append(pair)
+    me = lax.axis_index("tm").astype(jnp.int32)
+
+    def rows_of(core):
+        picked = []
+        for mask in masks:
+            span = pl.ds(pl.multiple_of((me ^ (mask ^ core)) * half, 8), half)
+            real, imag = turned_ref[0, span], turned_ref[1, span]
+            picked += [jnp.concatenate([real, imag], 1), jnp.concatenate([imag, -real], 1)]
+        return split(jnp.concatenate(picked, 0))
+
     for i in range(chunks):
         copies[i][0].wait()
-        real = solutions_ref[i, 0].T
-        imag = solutions_ref[i, 1].T
-        left = split(
-            jnp.concatenate(
-                [jnp.concatenate([real, imag], 0), jnp.concatenate([imag, -real], 0)], 1
-            )
-        )
+        for part in range(2):
+            turned_ref[part] = solutions_ref[i, part].T
+        left = rows_of(0)
+        keep_high_ref[i], keep_low_ref[i] = rows_of(1)
         copies[i][1].wait()
         right = split(evecs_ref[i].reshape(2 * step, modes))
         for ref, value in zip((high_ref, low_ref), right):
-            for part in range(2):
-                ref[part, i * step : (i + 1) * step] = value[part * step : (part + 1) * step]
-        value = dot3(left, right)
+            ref[i] = value
+        value = dot3(left, right).reshape(send_ref.shape)
         if i == 0:
-            total_ref[...] = value
+            send_ref[...] = value
         else:
-            total_ref[...] += value
-    me = lax.axis_index("tm").astype(jnp.int32)
-    for out, core in ((keep_ref, 1), (send_ref, 0)):
-        for m, mask in enumerate(masks):
-            block = me ^ (mask ^ core)
-            for part in range(2):
-                start = pl.multiple_of(part * cols + block * half, 8)
-                out[m, part * half : (part + 1) * half] = total_ref[pl.ds(start, half)]
+            send_ref[...] += value
+
+
+def keep_kernel(left_high_ref, left_low_ref, high_ref, low_ref, keep_ref):
+    total = None
+    for i in range(high_ref.shape[0]):
+        value = dot3((left_high_ref[i], left_low_ref[i]), (high_ref[i], low_ref[i]))
+        total = value if total is None else total + value
+    keep_ref[...] = total.reshape(keep_ref.shape)
 
 
 def project(evecs, solutions, masks):
@@ -84,19 +92,20 @@
     step = STEP if rows % STEP == 0 else rows
     chunks = rows // step
     out = jax.ShapeDtypeStruct((chips, block_rows, modes), F32)
-    held = jax.ShapeDtypeStruct((2, rows, modes), BF16)
+    held = jax.ShapeDtypeStruct((chunks, 2 * step, modes), BF16)
+    left = jax.ShapeDtypeStruct((chunks, chips * block_rows, 2 * step), BF16)
     return pl.pallas_call(
         functools.partial(project_kernel, masks),
         in_specs=[pl.BlockSpec(memory_space=pltpu.HBM)] * 2,
-        out_specs=[VMEM_SPEC] * 4,
+        out_specs=[VMEM_SPEC] * 5,
         scratch_shapes=[
             pltpu.VMEM((chunks, 2, step, modes), F32),
             pltpu.VMEM((chunks, 2, step, cols), F32),
-            pltpu.VMEM((2 * cols, modes), F32),
+            pltpu.VMEM((2, cols, step), F32),
             pltpu.SemaphoreType.DMA((2, chunks)),
         ],
-        out_shape=[out, out, held, held],
-        compiler_params=pltpu.CompilerParams(vmem_limit_bytes=54_000_000),
+        out_shape=[out, held, held, left, left],
+        compiler_params=pltpu.CompilerParams(vmem_limit_bytes=54000000),
         name="project",
     )(evecs, solutions)
 
@@ -143,9 +152,13 @@
 
 
 def turn_kernel(high_ref, low_ref, high_out, low_out):
-    for part in range(2):
-        high_out[part] = high_ref[part].T
-        low_out[part] = low_ref[part].T
+    chunks, rows, _ = high_ref.shape
+    step = rows // 2
+    for i in range(chunks):
+        for part in range(2):
+            span = slice(part * step, (part + 1) * step)
+            high_out[part, :, i * step : (i + 1) * step] = high_ref[i, span].T
+            low_out[part, :, i * step : (i + 1) * step] = low_ref[i, span].T
 
 
 def smear_kernel(high_ref, low_ref, mix_ref, *refs):
@@ -177,7 +190,7 @@
     width = solutions.shape[3] // n_time
     chips = n_time // 2
     masks = [0] + [2 * m + 1 for m in range(1, chips)]
-    keep, send, high, low = project(evecs, solutions, masks)
+    send, high, low, left_high, left_low = project(evecs, solutions, masks)
 
     def swap(value, mask, space=0):
         pairs = [
@@ -188,6 +201,14 @@
         return lax.ppermute(value, ("tm", "space"), pairs)
 
     recv = swap(send, 1)
+    keep = pl.pallas_call(
+        keep_kernel,
+        in_specs=[VMEM_SPEC] * 4,
+        out_specs=VMEM_SPEC,
+        out_shape=jax.ShapeDtypeStruct(send.shape, F32),
+        compiler_params=pltpu.CompilerParams(vmem_limit_bytes=8 << 20),
+        name="keep",
+    )(left_high, left_low, high, low)
     mix, weight = pl.pallas_call(
         functools.partial(mix_kernel, masks),
         in_specs=[VMEM_SPEC, VMEM_SPEC, SMEM_SPEC, SMEM_SPEC, SMEM_SPEC],

time: 21.5 us -> 21.1 us (0.981)
  waiting for transfers between devices: 6.91 us -> 6.4 us
    ppermute x9, waiting for transfers between devices: 6.91 us -> 6.4 us  [swap(): return lax.ppermute(value, ('tm', 'space'), pairs)]
    pallas_call x0 -> x1, Pallas kernels: none -> 0.48 us  [per_device(): pl.pallas_call(keep_kernel, in_specs=[VMEM_SPEC] * 4, out_specs=VMEM_SPEC...]
    pallas_call x1, Pallas kernels: 2.8 us -> 2.39 us  [project(): pl.pallas_call(functools.partial(project_kernel, masks), in_specs=[pl.Blo...]
  transfers between devices with their start and end apart: 9 -> 9, of which waited for: 6 -> 6; matrix products, arithmetic and copies ran while one was open for 0% -> 0% of each run, Pallas kernels for 5% -> 8%
where the time goes in v5:
time: 21.1 us; the launch traced here: 20.9 us
  starting transfers between devices  9.23 us (44%)
  waiting for transfers between devices  6.4 us (30%)
  Pallas kernels  5.18 us (25%)
    ppermute x9, starting transfers between devices, swap(): return lax.ppermute(value, ('tm', 'space'), pairs)  9.23 us
    ppermute x9, waiting for transfers between devices, swap(): return lax.ppermute(value, ('tm', 'space'), pairs)  6.4 us
    pallas_call x1, Pallas kernels, project(): pl.pallas_call(functools.partial(project_kernel, masks), in_specs=[pl.Blo...  2.39 us
    pallas_call x1, Pallas kernels, per_device(): pl.pallas_call(smear_kernel, in_specs=[VMEM_SPEC] * (n_space + 3), out_sp...  1.12 us
    pallas_call x1, Pallas kernels, per_device(): pl.pallas_call(functools.partial(mix_kernel, masks), in_specs=[VMEM_SPEC,...  0.71 us
    pallas_call x1, Pallas kernels, per_device(): pl.pallas_call(keep_kernel, in_specs=[VMEM_SPEC] * 4, out_specs=VMEM_SPEC...  0.48 us
    pallas_call x1, Pallas kernels, per_device(): pl.pallas_call(turn_kernel, in_specs=[VMEM_SPEC, VMEM_SPEC], out_specs=[V...  0.45 us
  transfers between devices with their start and end apart: 9, of which 6 were waited for; matrix products, arithmetic and copies ran while one was open for 0% of the time, Pallas kernels for 8%

profile of v5, /device:TPU:0, one launch (start us, length us, event | category | flops | bytes accessed | tf_op | source)
XLA Modules:
  0.0 20.9 jit_solution(12882543000044712576)
XLA Ops:
  0.0 2.4 %project.1 = (f32[4,32,256]{2,1,0:T(8,128)S(1)}, bf16[2,768,256]{2,1,0:T(8,128)(2,1)S(1)}, bf16[2,768,256]{2,1,0:T(8,128)(2,1)S(1)}, bf16[2,128,768]{2,1,0:T(8,128)(2,1)S(1)}, bf16[2,128,768]{2,1,0:T(8,128)(2,1)S(1)}) custom-call(f32[1,2,768,256]{3,2,1,0:T(8,128)} %evecs_hbm.1, f32[1,2,768,128]{3,2,1,0:T(8,128)} %solutions_hbm.1), custom_call_target="tpu_custom_call" | custom-call | tf_op jit(solution)/shard_map/project/pallas_call | solution.py:97
  2.4 0.6 %collective-permute-start.1 = (f32[4,32,256]{2,1,0:T(8,128)S(1)}, f32[4,32,256]{2,1,0:T(8,128)S(1)}, u32[]{:S(2)}, u32[]{:S(2)}) collective-permute-start(f32[4,32,256]{2,1,0:T(8,128)S(1)} %get-tuple-element.22), channel_id=1, source_target_pairs={{0,4},{1,5},{2,6},{3,7},{4,0},{5,1},{6,2},{7,3},{8,12},{9,13},{10,... | collective-permute-start | bytes 393224 | tf_op jit(solution)/shard_map/ppermute | solution.py:201
  3.0 0.0 copy-start
  3.0 0.0 copy-start.1
  3.0 0.0 copy-start.2
  3.0 0.0 copy-start.3
  3.0 0.0 copy-start.4
  3.0 0.5 %keep.1 = f32[4,32,256]{2,1,0:T(8,128)S(1)} custom-call(bf16[2,128,768]{2,1,0:T(8,128)(2,1)S(1)} %get-tuple-element.20.left_high_ref, bf16[2,128,768]{2,1,0:T(8,128)(2,1)S(1)} %get-tuple-element.21.left_low_ref, bf16[2,768,256]{2,1,0:T(8,128)(2,1)S(1)} %get-tuple-element.14.high_ref, bf16[2,768,256]{2,1,0:T(8,128)(2,1)S(1)} %get-tuple-element.15.low_ref), custom_call_target="tpu_custom_call" | custom-call | tf_op jit(solution)/shard_map/keep/pallas_call | solution.py:204
  3.5 0.5 %collective-permute-done.1 = f32[4,32,256]{2,1,0:T(8,128)S(1)} collective-permute-done((f32[4,32,256]{2,1,0:T(8,128)S(1)}, f32[4,32,256]{2,1,0:T(8,128)S(1)}, u32[]{:S(2)}, u32[]{:S(2)}) %collective-permute-start.1) | collective-permute-done | bytes 131104 | tf_op jit(solution)/shard_map/ppermute | solution.py:201
  4.0 3.6 %collective-permute-start.4 = (f32[2,32,256]{2,1,0:T(8,128)S(1)}, f32[2,32,256]{2,1,0:T(8,128)S(1)}, u32[]{:S(2)}, u32[]{:S(2)}) collective-permute-start(f32[2,32,256]{2,1,0:T(8,128)S(1)} %pad_maximum_fusion.2), channel_id=1, source_target_pairs={{0,28},{1,29},{2,30},{3,31},{4,24},{5,25},{6,26},{7,27},{8,20},{9,... | collective-permute-start | bytes 196616 | tf_op jit(solution)/shard_map/ppermute | solution.py:201
  7.6 0.5 %collective-permute-start.3 = (f32[2,32,256]{2,1,0:T(8,128)S(1)}, f32[2,32,256]{2,1,0:T(8,128)S(1)}, u32[]{:S(2)}, u32[]{:S(2)}) collective-permute-start(f32[2,32,256]{2,1,0:T(8,128)S(1)} %pad_maximum_fusion.1), channel_id=1, source_target_pairs={{0,20},{1,21},{2,22},{3,23},{4,16},{5,17},{6,18},{7,19},{8,28},{9,... | collective-permute-start | bytes 196616 | tf_op jit(solution)/shard_map/ppermute | solution.py:201
  8.1 0.1 collective-permute-start.2
  8.2 0.0 copy-done
  8.2 0.0 copy-done.1
  8.2 0.0 copy-done.2
  8.2 0.0 copy-done.3
  8.2 0.0 copy-done.4
  8.2 0.7 %mix.1 = (f32[32,32]{1,0:T(8,128)S(1)}, f32[8,256]{1,0:T(8,128)S(1)}) custom-call(f32[1,2,4,256]{3,2,1,0:T(4,128)S(1)} %copy-done, f32[1,2,4,256]{3,2,1,0:T(4,128)S(1)} %copy-done.1, s32[1,4]{1,0:T(1,128)S(1)} %copy-done.2, s32[1,4]{1,0:T(1,128)S(1)} %copy-done.3, f32[1,8]{1,0:T(1,128)S(1)} %bitcast.1), custom_call_target="tpu_custom_call" | custom-call | tf_op jit(solution)/shard_map/mix/pallas_call | solution.py:212
  9.0 0.2 collective-permute-start
  9.1 1.0 %collective-permute-done.weight_ref = f32[8,256]{1,0:T(8,128)S(1)} collective-permute-done((f32[8,256]{1,0:T(8,128)S(1)}, f32[8,256]{1,0:T(8,128)S(1)}, u32[]{:S(2)}, u32[]{:S(2)}) %collective-permute-start) | collective-permute-done | bytes 8224 | tf_op jit(solution)/shard_map/ppermute | solution.py:201
  10.1 0.0 collective-permute-done.4.refs_2_
  10.1 1.3 %collective-permute-done.3.refs_1_ = f32[2,32,256]{2,1,0:T(8,128)S(1)} collective-permute-done((f32[2,32,256]{2,1,0:T(8,128)S(1)}, f32[2,32,256]{2,1,0:T(8,128)S(1)}, u32[]{:S(2)}, u32[]{:S(2)}) %collective-permute-start.3) | collective-permute-done | bytes 65568 | tf_op jit(solution)/shard_map/ppermute | solution.py:201
  11.4 0.7 %collective-permute-done.2.refs_0_ = f32[2,32,256]{2,1,0:T(8,128)S(1)} collective-permute-done((f32[2,32,256]{2,1,0:T(8,128)S(1)}, f32[2,32,256]{2,1,0:T(8,128)S(1)}, u32[]{:S(2)}, u32[]{:S(2)}) %collective-permute-start.2) | collective-permute-done | bytes 65568 | tf_op jit(solution)/shard_map/ppermute | solution.py:201
  12.2 3.4 %collective-permute-start.5 = (f32[32,256]{1,0:T(8,128)S(1)}, f32[32,256]{1,0:T(8,128)S(1)}, u32[]{:S(2)}, u32[]{:S(2)}) collective-permute-start(f32[32,256]{1,0:T(8,128)S(1)} %recombine.1), channel_id=1, source_target_pairs={{0,7},{1,6},{2,5},{3,4},{4,3},{5,2},{6,1},{7,0},{8,15},{9,14},{10,... | collective-permute-start | bytes 98312 | tf_op jit(solution)/shard_map/ppermute | solution.py:201
  15.6 0.0 collective-permute-start.6
  15.6 0.6 %collective-permute-start.7 = (f32[32,256]{1,0:T(8,128)S(1)}, f32[32,256]{1,0:T(8,128)S(1)}, u32[]{:S(2)}, u32[]{:S(2)}) collective-permute-start(f32[32,256]{1,0:T(8,128)S(1)} %recombine.1), channel_id=1, source_target_pairs={{0,5},{1,4},{2,7},{3,6},{4,1},{5,0},{6,3},{7,2},{8,13},{9,12},{10,... | collective-permute-start | bytes 98312 | tf_op jit(solution)/shard_map/ppermute | solution.py:201
  16.2 0.3 %collective-permute-start.8 = (f32[32,256]{1,0:T(8,128)S(1)}, f32[32,256]{1,0:T(8,128)S(1)}, u32[]{:S(2)}, u32[]{:S(2)}) collective-permute-start(f32[32,256]{1,0:T(8,128)S(1)} %recombine.1), channel_id=1, source_target_pairs={{0,4},{1,5},{2,6},{3,7},{4,0},{5,1},{6,2},{7,3},{8,12},{9,13},{10,... | collective-permute-start | bytes 98312 | tf_op jit(solution)/shard_map/ppermute | solution.py:201
  16.4 0.5 %turn.1 = (bf16[2,256,768]{2,1,0:T(8,128)(2,1)S(1)}, bf16[2,256,768]{2,1,0:T(8,128)(2,1)S(1)}) custom-call(bf16[2,768,256]{2,1,0:T(8,128)(2,1)S(1)} %get-tuple-element.14.high_ref, bf16[2,768,256]{2,1,0:T(8,128)(2,1)S(1)} %get-tuple-element.15.low_ref), custom_call_target="tpu_custom_call" | custom-call | tf_op jit(solution)/shard_map/turn/pallas_call | solution.py:225
  16.9 0.5 %collective-permute-done.5.refs_0_ = f32[32,256]{1,0:T(8,128)S(1)} collective-permute-done((f32[32,256]{1,0:T(8,128)S(1)}, f32[32,256]{1,0:T(8,128)S(1)}, u32[]{:S(2)}, u32[]{:S(2)}) %collective-permute-start.5) | collective-permute-done | bytes 32800 | tf_op jit(solution)/shard_map/ppermute | solution.py:201
  17.4 2.5 %collective-permute-done.6.refs_1_ = f32[32,256]{1,0:T(8,128)S(1)} collective-permute-done((f32[32,256]{1,0:T(8,128)S(1)}, f32[32,256]{1,0:T(8,128)S(1)}, u32[]{:S(2)}, u32[]{:S(2)}) %collective-permute-start.6) | collective-permute-done | bytes 32800 | tf_op jit(solution)/shard_map/ppermute | solution.py:201
  19.8 0.0 collective-permute-done.7.refs_2_
  19.8 0.0 collective-permute-done.8.refs_3_
  19.8 1.1 %smear.1 = f32[1,2,16,768]{3,2,1,0:T(8,128)} custom-call(bf16[2,256,768]{2,1,0:T(8,128)(2,1)S(1)} %get-tuple-element.16.high_ref, bf16[2,256,768]{2,1,0:T(8,128)(2,1)S(1)} %get-tuple-element.17.low_ref, f32[32,32]{1,0:T(8,128)S(1)} %get-tuple-element.18.mix_ref, f32[32,256]{1,0:T(8,128)S(1)} %collective-permute-done.5.refs_0_, ...), custom_call_target="tpu_custom_call" | custom-call | tf_op jit(solution)/shard_map/smear/pallas_call | solution.py:244
  (6 shorter events, 0.1 us)
Async XLA Ops:
  2.4 1.5 %collective-permute-start.1 = (f32[4,32,256]{2,1,0:T(8,128)S(1)}, f32[4,32,256]{2,1,0:T(8,128)S(1)}, u32[]{:S(2)}, u32[]{:S(2)}) collective-permute-start(f32[4,32,256]{2,1,0:T(8,128)S(1)} %get-tuple-element.22), channel_id=1, source_target_pairs={{0,4},{1,5},{2,6},{3,7},{4,0},{5,1},{6,2},{7,3},{8,12},{9,13},{10,... | collective-permute-start | bytes 393224 | tf_op jit(solution)/shard_map/ppermute | solution.py:201
  3.0 5.3 %copy-start = (f32[1,2,4,256]{3,2,1,0:T(4,128)S(1)}, f32[1,2,4,256]{3,2,1,0:T(4,128)}, u32[]{:S(2)}) copy-start(f32[1,2,4,256]{3,2,1,0:T(4,128)} %noise_ref.1) | copy-start | bytes 24580
  3.0 5.3 %copy-start.1 = (f32[1,2,4,256]{3,2,1,0:T(4,128)S(1)}, f32[1,2,4,256]{3,2,1,0:T(4,128)}, u32[]{:S(2)}) copy-start(f32[1,2,4,256]{3,2,1,0:T(4,128)} %probe_ref.1) | copy-start | bytes 24580
  3.0 5.3 %copy-start.2 = (s32[1,4]{1,0:T(1,128)S(1)}, s32[1,4]{1,0:T(1,128)}, u32[]{:S(2)}) copy-start(s32[1,4]{1,0:T(1,128)} %spin_ref.1) | copy-start | bytes 52
  3.0 5.3 %copy-start.3 = (s32[1,4]{1,0:T(1,128)S(1)}, s32[1,4]{1,0:T(1,128)}, u32[]{:S(2)}) copy-start(s32[1,4]{1,0:T(1,128)} %lace_ref.1) | copy-start | bytes 52
  3.0 5.3 %copy-start.4 = (f32[8,1]{0,1:T(1,128)S(1)}, f32[8,1]{0,1:T(1,128)}, u32[]{:S(2)}) copy-start(f32[8,1]{0,1:T(1,128)} %param.9) | copy-start | bytes 100
  4.0 6.2 %collective-permute-start.4 = (f32[2,32,256]{2,1,0:T(8,128)S(1)}, f32[2,32,256]{2,1,0:T(8,128)S(1)}, u32[]{:S(2)}, u32[]{:S(2)}) collective-permute-start(f32[2,32,256]{2,1,0:T(8,128)S(1)} %pad_maximum_fusion.2), channel_id=1, source_target_pairs={{0,28},{1,29},{2,30},{3,31},{4,24},{5,25},{6,26},{7,27},{8,20},{9,... | collective-permute-start | bytes 196616 | tf_op jit(solution)/shard_map/ppermute | solution.py:201
  7.6 3.9 %collective-permute-start.3 = (f32[2,32,256]{2,1,0:T(8,128)S(1)}, f32[2,32,256]{2,1,0:T(8,128)S(1)}, u32[]{:S(2)}, u32[]{:S(2)}) collective-permute-start(f32[2,32,256]{2,1,0:T(8,128)S(1)} %pad_maximum_fusion.1), channel_id=1, source_target_pairs={{0,20},{1,21},{2,22},{3,23},{4,16},{5,17},{6,18},{7,19},{8,28},{9,... | collective-permute-start | bytes 196616 | tf_op jit(solution)/shard_map/ppermute | solution.py:201
  8.1 4.1 %collective-permute-start.2 = (f32[2,32,256]{2,1,0:T(8,128)S(1)}, f32[2,32,256]{2,1,0:T(8,128)S(1)}, u32[]{:S(2)}, u32[]{:S(2)}) collective-permute-start(f32[2,32,256]{2,1,0:T(8,128)S(1)} %pad_maximum_fusion), channel_id=1, source_target_pairs={{0,12},{1,13},{2,14},{3,15},{4,8},{5,9},{6,10},{7,11},{8,4},{9,5},... | collective-permute-start | bytes 196616 | tf_op jit(solution)/shard_map/ppermute | solution.py:201
  9.0 1.2 %collective-permute-start = (f32[8,256]{1,0:T(8,128)S(1)}, f32[8,256]{1,0:T(8,128)S(1)}, u32[]{:S(2)}, u32[]{:S(2)}) collective-permute-start(f32[8,256]{1,0:T(8,128)S(1)} %get-tuple-element.19), channel_id=1, source_target_pairs={{0,4},{1,5},{2,6},{3,7},{4,0},{5,1},{6,2},{7,3},{8,12},{9,13},{10,... | collective-permute-start | bytes 24584 | tf_op jit(solution)/shard_map/ppermute | solution.py:201
  12.2 5.2 %collective-permute-start.5 = (f32[32,256]{1,0:T(8,128)S(1)}, f32[32,256]{1,0:T(8,128)S(1)}, u32[]{:S(2)}, u32[]{:S(2)}) collective-permute-start(f32[32,256]{1,0:T(8,128)S(1)} %recombine.1), channel_id=1, source_target_pairs={{0,7},{1,6},{2,5},{3,4},{4,3},{5,2},{6,1},{7,0},{8,15},{9,14},{10,... | collective-permute-start | bytes 98312 | tf_op jit(solution)/shard_map/ppermute | solution.py:201
  15.6 4.2 %collective-permute-start.6 = (f32[32,256]{1,0:T(8,128)S(1)}, f32[32,256]{1,0:T(8,128)S(1)}, u32[]{:S(2)}, u32[]{:S(2)}) collective-permute-start(f32[32,256]{1,0:T(8,128)S(1)} %recombine.1), channel_id=1, source_target_pairs={{0,6},{1,7},{2,4},{3,5},{4,2},{5,3},{6,0},{7,1},{8,14},{9,15},{10,... | collective-permute-start | bytes 98312 | tf_op jit(solution)/shard_map/ppermute | solution.py:201
  15.6 4.2 %collective-permute-start.7 = (f32[32,256]{1,0:T(8,128)S(1)}, f32[32,256]{1,0:T(8,128)S(1)}, u32[]{:S(2)}, u32[]{:S(2)}) collective-permute-start(f32[32,256]{1,0:T(8,128)S(1)} %recombine.1), channel_id=1, source_target_pairs={{0,5},{1,4},{2,7},{3,6},{4,1},{5,0},{6,3},{7,2},{8,13},{9,12},{10,... | collective-permute-start | bytes 98312 | tf_op jit(solution)/shard_map/ppermute | solution.py:201
  16.2 3.6 %collective-permute-start.8 = (f32[32,256]{1,0:T(8,128)S(1)}, f32[32,256]{1,0:T(8,128)S(1)}, u32[]{:S(2)}, u32[]{:S(2)}) collective-permute-start(f32[32,256]{1,0:T(8,128)S(1)} %recombine.1), channel_id=1, source_target_pairs={{0,4},{1,5},{2,6},{3,7},{4,0},{5,1},{6,2},{7,3},{8,12},{9,13},{10,... | collective-permute-start | bytes 98312 | tf_op jit(solution)/shard_map/ppermute | solution.py:201

commit v6 on v5

--- a/solution.py
+++ b/solution.py
@@ -34,21 +34,17 @@
 
 def project_kernel(
     masks, evecs_hbm, solutions_hbm, send_ref, high_ref, low_ref, keep_high_ref, keep_low_ref,
-    evecs_ref, solutions_ref, turned_ref, sems
+    evecs_ref, solutions_ref, turned_ref, left_ref, sems
 ):
     chunks, _, step, modes = evecs_ref.shape
     cols = solutions_ref.shape[3]
     half = cols // (2 * len(masks))
     copies = []
-    for i in range(chunks):
-        rows = pl.ds(i * step, step)
-        pair = (
-            pltpu.make_async_copy(solutions_hbm.at[0, :, rows], solutions_ref.at[i], sems.at[0, i]),
-            pltpu.make_async_copy(evecs_hbm.at[0, :, rows], evecs_ref.at[i], sems.at[1, i]),
-        )
-        for copy in pair:
-            copy.start()
-        copies.append(pair)
+    for ref, source, sem in ((solutions_ref, solutions_hbm, 0), (evecs_ref, evecs_hbm, 1)):
+        for i in range(chunks):
+            rows = pl.ds(i * step, step)
+            copies.append(pltpu.make_async_copy(source.at[0, :, rows], ref.at[i], sems.at[sem, i]))
+            copies[-1].start()
     me = lax.axis_index("tm").astype(jnp.int32)
 
     def rows_of(core):
@@ -60,12 +56,14 @@
         return split(jnp.concatenate(picked, 0))
 
     for i in range(chunks):
-        copies[i][0].wait()
+        copies[i].wait()
         for part in range(2):
             turned_ref[part] = solutions_ref[i, part].T
-        left = rows_of(0)
+        left_ref[i, 0], left_ref[i, 1] = rows_of(0)
         keep_high_ref[i], keep_low_ref[i] = rows_of(1)
-        copies[i][1].wait()
+    for i in range(chunks):
+        left = left_ref[i, 0], left_ref[i, 1]
+        copies[chunks + i].wait()
         right = split(evecs_ref[i].reshape(2 * step, modes))
         for ref, value in zip((high_ref, low_ref), right):
             ref[i] = value
@@ -102,6 +100,7 @@
             pltpu.VMEM((chunks, 2, step, modes), F32),
             pltpu.VMEM((chunks, 2, step, cols), F32),
             pltpu.VMEM((2, cols, step), F32),
+            pltpu.VMEM((chunks, 2, chips * block_rows, 2 * step), BF16),
             pltpu.SemaphoreType.DMA((2, chunks)),
         ],
         out_shape=[out, held, held, left, left],

time: 21.1 us -> 21.1 us (level)
  no operation moved by 1% of the time
where the time goes in v6:
time: 21.1 us; the launch traced here: 20.9 us
  starting transfers between devices  9.23 us (44%)
  waiting for transfers between devices  6.4 us (30%)
  Pallas kernels  5.16 us (24%)
    ppermute x9, starting transfers between devices, swap(): return lax.ppermute(value, ('tm', 'space'), pairs)  9.23 us
    ppermute x9, waiting for transfers between devices, swap(): return lax.ppermute(value, ('tm', 'space'), pairs)  6.4 us
    pallas_call x1, Pallas kernels, project(): pl.pallas_call(functools.partial(project_kernel, masks), in_specs=[pl.Blo...  2.38 us
    pallas_call x1, Pallas kernels, per_device(): pl.pallas_call(smear_kernel, in_specs=[VMEM_SPEC] * (n_space + 3), out_sp...  1.12 us
    pallas_call x1, Pallas kernels, per_device(): pl.pallas_call(functools.partial(mix_kernel, masks), in_specs=[VMEM_SPEC,...  0.71 us
    pallas_call x1, Pallas kernels, per_device(): pl.pallas_call(keep_kernel, in_specs=[VMEM_SPEC] * 4, out_specs=VMEM_SPEC...  0.48 us
    pallas_call x1, Pallas kernels, per_device(): pl.pallas_call(turn_kernel, in_specs=[VMEM_SPEC, VMEM_SPEC], out_specs=[V...  0.45 us
  transfers between devices with their start and end apart: 9, of which 6 were waited for; matrix products, arithmetic and copies ran while one was open for 0% of the time, Pallas kernels for 8%

profile of v6, /device:TPU:0, one launch (start us, length us, event | category | flops | bytes accessed | tf_op | source)
XLA Modules:
  0.0 20.9 jit_solution(7739733609308060088)
XLA Ops:
  0.0 2.4 %project.1 = (f32[4,32,256]{2,1,0:T(8,128)S(1)}, bf16[2,768,256]{2,1,0:T(8,128)(2,1)S(1)}, bf16[2,768,256]{2,1,0:T(8,128)(2,1)S(1)}, bf16[2,128,768]{2,1,0:T(8,128)(2,1)S(1)}, bf16[2,128,768]{2,1,0:T(8,128)(2,1)S(1)}) custom-call(f32[1,2,768,256]{3,2,1,0:T(8,128)} %evecs_hbm.1, f32[1,2,768,128]{3,2,1,0:T(8,128)} %solutions_hbm.1), custom_call_target="tpu_custom_call" | custom-call | tf_op jit(solution)/shard_map/project/pallas_call | solution.py:95
  2.4 0.6 %collective-permute-start.1 = (f32[4,32,256]{2,1,0:T(8,128)S(1)}, f32[4,32,256]{2,1,0:T(8,128)S(1)}, u32[]{:S(2)}, u32[]{:S(2)}) collective-permute-start(f32[4,32,256]{2,1,0:T(8,128)S(1)} %get-tuple-element.22), channel_id=1, source_target_pairs={{0,4},{1,5},{2,6},{3,7},{4,0},{5,1},{6,2},{7,3},{8,12},{9,13},{10,... | collective-permute-start | bytes 393224 | tf_op jit(solution)/shard_map/ppermute | solution.py:200
  2.9 0.0 copy-start
  2.9 0.0 copy-start.1
  3.0 0.0 copy-start.2
  3.0 0.0 copy-start.3
  3.0 0.0 copy-start.4
  3.0 0.5 %keep.1 = f32[4,32,256]{2,1,0:T(8,128)S(1)} custom-call(bf16[2,128,768]{2,1,0:T(8,128)(2,1)S(1)} %get-tuple-element.20.left_high_ref, bf16[2,128,768]{2,1,0:T(8,128)(2,1)S(1)} %get-tuple-element.21.left_low_ref, bf16[2,768,256]{2,1,0:T(8,128)(2,1)S(1)} %get-tuple-element.14.high_ref, bf16[2,768,256]{2,1,0:T(8,128)(2,1)S(1)} %get-tuple-element.15.low_ref), custom_call_target="tpu_custom_call" | custom-call | tf_op jit(solution)/shard_map/keep/pallas_call | solution.py:203
  3.5 0.5 %collective-permute-done.1 = f32[4,32,256]{2,1,0:T(8,128)S(1)} collective-permute-done((f32[4,32,256]{2,1,0:T(8,128)S(1)}, f32[4,32,256]{2,1,0:T(8,128)S(1)}, u32[]{:S(2)}, u32[]{:S(2)}) %collective-permute-start.1) | collective-permute-done | bytes 131104 | tf_op jit(solution)/shard_map/ppermute | solution.py:200
  4.0 3.6 %collective-permute-start.4 = (f32[2,32,256]{2,1,0:T(8,128)S(1)}, f32[2,32,256]{2,1,0:T(8,128)S(1)}, u32[]{:S(2)}, u32[]{:S(2)}) collective-permute-start(f32[2,32,256]{2,1,0:T(8,128)S(1)} %pad_maximum_fusion.2), channel_id=1, source_target_pairs={{0,28},{1,29},{2,30},{3,31},{4,24},{5,25},{6,26},{7,27},{8,20},{9,... | collective-permute-start | bytes 196616 | tf_op jit(solution)/shard_map/ppermute | solution.py:200
  7.6 0.5 %collective-permute-start.3 = (f32[2,32,256]{2,1,0:T(8,128)S(1)}, f32[2,32,256]{2,1,0:T(8,128)S(1)}, u32[]{:S(2)}, u32[]{:S(2)}) collective-permute-start(f32[2,32,256]{2,1,0:T(8,128)S(1)} %pad_maximum_fusion.1), channel_id=1, source_target_pairs={{0,20},{1,21},{2,22},{3,23},{4,16},{5,17},{6,18},{7,19},{8,28},{9,... | collective-permute-start | bytes 196616 | tf_op jit(solution)/shard_map/ppermute | solution.py:200
  8.1 0.1 collective-permute-start.2
  8.2 0.0 copy-done
  8.2 0.0 copy-done.1
  8.2 0.0 copy-done.2
  8.2 0.0 copy-done.3
  8.2 0.0 copy-done.4
  8.2 0.7 %mix.1 = (f32[32,32]{1,0:T(8,128)S(1)}, f32[8,256]{1,0:T(8,128)S(1)}) custom-call(f32[1,2,4,256]{3,2,1,0:T(4,128)S(1)} %copy-done, f32[1,2,4,256]{3,2,1,0:T(4,128)S(1)} %copy-done.1, s32[1,4]{1,0:T(1,128)S(1)} %copy-done.2, s32[1,4]{1,0:T(1,128)S(1)} %copy-done.3, f32[1,8]{1,0:T(1,128)S(1)} %bitcast.1), custom_call_target="tpu_custom_call" | custom-call | tf_op jit(solution)/shard_map/mix/pallas_call | solution.py:211
  8.9 0.2 collective-permute-start
  9.1 1.0 %collective-permute-done.weight_ref = f32[8,256]{1,0:T(8,128)S(1)} collective-permute-done((f32[8,256]{1,0:T(8,128)S(1)}, f32[8,256]{1,0:T(8,128)S(1)}, u32[]{:S(2)}, u32[]{:S(2)}) %collective-permute-start) | collective-permute-done | bytes 8224 | tf_op jit(solution)/shard_map/ppermute | solution.py:200
  10.1 0.0 collective-permute-done.4.refs_2_
  10.1 1.3 %collective-permute-done.3.refs_1_ = f32[2,32,256]{2,1,0:T(8,128)S(1)} collective-permute-done((f32[2,32,256]{2,1,0:T(8,128)S(1)}, f32[2,32,256]{2,1,0:T(8,128)S(1)}, u32[]{:S(2)}, u32[]{:S(2)}) %collective-permute-start.3) | collective-permute-done | bytes 65568 | tf_op jit(solution)/shard_map/ppermute | solution.py:200
  11.4 0.7 %collective-permute-done.2.refs_0_ = f32[2,32,256]{2,1,0:T(8,128)S(1)} collective-permute-done((f32[2,32,256]{2,1,0:T(8,128)S(1)}, f32[2,32,256]{2,1,0:T(8,128)S(1)}, u32[]{:S(2)}, u32[]{:S(2)}) %collective-permute-start.2) | collective-permute-done | bytes 65568 | tf_op jit(solution)/shard_map/ppermute | solution.py:200
  12.1 3.4 %collective-permute-start.5 = (f32[32,256]{1,0:T(8,128)S(1)}, f32[32,256]{1,0:T(8,128)S(1)}, u32[]{:S(2)}, u32[]{:S(2)}) collective-permute-start(f32[32,256]{1,0:T(8,128)S(1)} %recombine.1), channel_id=1, source_target_pairs={{0,7},{1,6},{2,5},{3,4},{4,3},{5,2},{6,1},{7,0},{8,15},{9,14},{10,... | collective-permute-start | bytes 98312 | tf_op jit(solution)/shard_map/ppermute | solution.py:200
  15.6 0.0 collective-permute-start.6
  15.6 0.6 %collective-permute-start.7 = (f32[32,256]{1,0:T(8,128)S(1)}, f32[32,256]{1,0:T(8,128)S(1)}, u32[]{:S(2)}, u32[]{:S(2)}) collective-permute-start(f32[32,256]{1,0:T(8,128)S(1)} %recombine.1), channel_id=1, source_target_pairs={{0,5},{1,4},{2,7},{3,6},{4,1},{5,0},{6,3},{7,2},{8,13},{9,12},{10,... | collective-permute-start | bytes 98312 | tf_op jit(solution)/shard_map/ppermute | solution.py:200
  16.2 0.3 %collective-permute-start.8 = (f32[32,256]{1,0:T(8,128)S(1)}, f32[32,256]{1,0:T(8,128)S(1)}, u32[]{:S(2)}, u32[]{:S(2)}) collective-permute-start(f32[32,256]{1,0:T(8,128)S(1)} %recombine.1), channel_id=1, source_target_pairs={{0,4},{1,5},{2,6},{3,7},{4,0},{5,1},{6,2},{7,3},{8,12},{9,13},{10,... | collective-permute-start | bytes 98312 | tf_op jit(solution)/shard_map/ppermute | solution.py:200
  16.4 0.5 %turn.1 = (bf16[2,256,768]{2,1,0:T(8,128)(2,1)S(1)}, bf16[2,256,768]{2,1,0:T(8,128)(2,1)S(1)}) custom-call(bf16[2,768,256]{2,1,0:T(8,128)(2,1)S(1)} %get-tuple-element.14.high_ref, bf16[2,768,256]{2,1,0:T(8,128)(2,1)S(1)} %get-tuple-element.15.low_ref), custom_call_target="tpu_custom_call" | custom-call | tf_op jit(solution)/shard_map/turn/pallas_call | solution.py:224
  16.9 0.5 %collective-permute-done.5.refs_0_ = f32[32,256]{1,0:T(8,128)S(1)} collective-permute-done((f32[32,256]{1,0:T(8,128)S(1)}, f32[32,256]{1,0:T(8,128)S(1)}, u32[]{:S(2)}, u32[]{:S(2)}) %collective-permute-start.5) | collective-permute-done | bytes 32800 | tf_op jit(solution)/shard_map/ppermute | solution.py:200
  17.4 2.5 %collective-permute-done.6.refs_1_ = f32[32,256]{1,0:T(8,128)S(1)} collective-permute-done((f32[32,256]{1,0:T(8,128)S(1)}, f32[32,256]{1,0:T(8,128)S(1)}, u32[]{:S(2)}, u32[]{:S(2)}) %collective-permute-start.6) | collective-permute-done | bytes 32800 | tf_op jit(solution)/shard_map/ppermute | solution.py:200
  19.8 0.0 collective-permute-done.7.refs_2_
  19.8 0.0 collective-permute-done.8.refs_3_
  19.8 1.1 %smear.1 = f32[1,2,16,768]{3,2,1,0:T(8,128)} custom-call(bf16[2,256,768]{2,1,0:T(8,128)(2,1)S(1)} %get-tuple-element.16.high_ref, bf16[2,256,768]{2,1,0:T(8,128)(2,1)S(1)} %get-tuple-element.17.low_ref, f32[32,32]{1,0:T(8,128)S(1)} %get-tuple-element.18.mix_ref, f32[32,256]{1,0:T(8,128)S(1)} %collective-permute-done.5.refs_0_, ...), custom_call_target="tpu_custom_call" | custom-call | tf_op jit(solution)/shard_map/smear/pallas_call | solution.py:243
  (6 shorter events, 0.1 us)
Async XLA Ops:
  2.4 1.5 %collective-permute-start.1 = (f32[4,32,256]{2,1,0:T(8,128)S(1)}, f32[4,32,256]{2,1,0:T(8,128)S(1)}, u32[]{:S(2)}, u32[]{:S(2)}) collective-permute-start(f32[4,32,256]{2,1,0:T(8,128)S(1)} %get-tuple-element.22), channel_id=1, source_target_pairs={{0,4},{1,5},{2,6},{3,7},{4,0},{5,1},{6,2},{7,3},{8,12},{9,13},{10,... | collective-permute-start | bytes 393224 | tf_op jit(solution)/shard_map/ppermute | solution.py:200
  2.9 5.3 %copy-start = (f32[1,2,4,256]{3,2,1,0:T(4,128)S(1)}, f32[1,2,4,256]{3,2,1,0:T(4,128)}, u32[]{:S(2)}) copy-start(f32[1,2,4,256]{3,2,1,0:T(4,128)} %noise_ref.1) | copy-start | bytes 24580
  2.9 5.3 %copy-start.1 = (f32[1,2,4,256]{3,2,1,0:T(4,128)S(1)}, f32[1,2,4,256]{3,2,1,0:T(4,128)}, u32[]{:S(2)}) copy-start(f32[1,2,4,256]{3,2,1,0:T(4,128)} %probe_ref.1) | copy-start | bytes 24580
  3.0 5.3 %copy-start.2 = (s32[1,4]{1,0:T(1,128)S(1)}, s32[1,4]{1,0:T(1,128)}, u32[]{:S(2)}) copy-start(s32[1,4]{1,0:T(1,128)} %spin_ref.1) | copy-start | bytes 52
  3.0 5.3 %copy-start.3 = (s32[1,4]{1,0:T(1,128)S(1)}, s32[1,4]{1,0:T(1,128)}, u32[]{:S(2)}) copy-start(s32[1,4]{1,0:T(1,128)} %lace_ref.1) | copy-start | bytes 52
  3.0 5.3 %copy-start.4 = (f32[8,1]{0,1:T(1,128)S(1)}, f32[8,1]{0,1:T(1,128)}, u32[]{:S(2)}) copy-start(f32[8,1]{0,1:T(1,128)} %param.9) | copy-start | bytes 100
  4.0 6.2 %collective-permute-start.4 = (f32[2,32,256]{2,1,0:T(8,128)S(1)}, f32[2,32,256]{2,1,0:T(8,128)S(1)}, u32[]{:S(2)}, u32[]{:S(2)}) collective-permute-start(f32[2,32,256]{2,1,0:T(8,128)S(1)} %pad_maximum_fusion.2), channel_id=1, source_target_pairs={{0,28},{1,29},{2,30},{3,31},{4,24},{5,25},{6,26},{7,27},{8,20},{9,... | collective-permute-start | bytes 196616 | tf_op jit(solution)/shard_map/ppermute | solution.py:200
  7.6 3.9 %collective-permute-start.3 = (f32[2,32,256]{2,1,0:T(8,128)S(1)}, f32[2,32,256]{2,1,0:T(8,128)S(1)}, u32[]{:S(2)}, u32[]{:S(2)}) collective-permute-start(f32[2,32,256]{2,1,0:T(8,128)S(1)} %pad_maximum_fusion.1), channel_id=1, source_target_pairs={{0,20},{1,21},{2,22},{3,23},{4,16},{5,17},{6,18},{7,19},{8,28},{9,... | collective-permute-start | bytes 196616 | tf_op jit(solution)/shard_map/ppermute | solution.py:200
  8.1 4.1 %collective-permute-start.2 = (f32[2,32,256]{2,1,0:T(8,128)S(1)}, f32[2,32,256]{2,1,0:T(8,128)S(1)}, u32[]{:S(2)}, u32[]{:S(2)}) collective-permute-start(f32[2,32,256]{2,1,0:T(8,128)S(1)} %pad_maximum_fusion), channel_id=1, source_target_pairs={{0,12},{1,13},{2,14},{3,15},{4,8},{5,9},{6,10},{7,11},{8,4},{9,5},... | collective-permute-start | bytes 196616 | tf_op jit(solution)/shard_map/ppermute | solution.py:200
  8.9 1.2 %collective-permute-start = (f32[8,256]{1,0:T(8,128)S(1)}, f32[8,256]{1,0:T(8,128)S(1)}, u32[]{:S(2)}, u32[]{:S(2)}) collective-permute-start(f32[8,256]{1,0:T(8,128)S(1)} %get-tuple-element.19), channel_id=1, source_target_pairs={{0,4},{1,5},{2,6},{3,7},{4,0},{5,1},{6,2},{7,3},{8,12},{9,13},{10,... | collective-permute-start | bytes 24584 | tf_op jit(solution)/shard_map/ppermute | solution.py:200
  12.1 5.2 %collective-permute-start.5 = (f32[32,256]{1,0:T(8,128)S(1)}, f32[32,256]{1,0:T(8,128)S(1)}, u32[]{:S(2)}, u32[]{:S(2)}) collective-permute-start(f32[32,256]{1,0:T(8,128)S(1)} %recombine.1), channel_id=1, source_target_pairs={{0,7},{1,6},{2,5},{3,4},{4,3},{5,2},{6,1},{7,0},{8,15},{9,14},{10,... | collective-permute-start | bytes 98312 | tf_op jit(solution)/shard_map/ppermute | solution.py:200
  15.6 4.2 %collective-permute-start.6 = (f32[32,256]{1,0:T(8,128)S(1)}, f32[32,256]{1,0:T(8,128)S(1)}, u32[]{:S(2)}, u32[]{:S(2)}) collective-permute-start(f32[32,256]{1,0:T(8,128)S(1)} %recombine.1), channel_id=1, source_target_pairs={{0,6},{1,7},{2,4},{3,5},{4,2},{5,3},{6,0},{7,1},{8,14},{9,15},{10,... | collective-permute-start | bytes 98312 | tf_op jit(solution)/shard_map/ppermute | solution.py:200
  15.6 4.2 %collective-permute-start.7 = (f32[32,256]{1,0:T(8,128)S(1)}, f32[32,256]{1,0:T(8,128)S(1)}, u32[]{:S(2)}, u32[]{:S(2)}) collective-permute-start(f32[32,256]{1,0:T(8,128)S(1)} %recombine.1), channel_id=1, source_target_pairs={{0,5},{1,4},{2,7},{3,6},{4,1},{5,0},{6,3},{7,2},{8,13},{9,12},{10,... | collective-permute-start | bytes 98312 | tf_op jit(solution)/shard_map/ppermute | solution.py:200
  16.2 3.6 %collective-permute-start.8 = (f32[32,256]{1,0:T(8,128)S(1)}, f32[32,256]{1,0:T(8,128)S(1)}, u32[]{:S(2)}, u32[]{:S(2)}) collective-permute-start(f32[32,256]{1,0:T(8,128)S(1)} %recombine.1), channel_id=1, source_target_pairs={{0,4},{1,5},{2,6},{3,7},{4,0},{5,1},{6,2},{7,3},{8,12},{9,13},{10,... | collective-permute-start | bytes 98312 | tf_op jit(solution)/shard_map/ppermute | solution.py:200
